TPU v7x, 256 devices: a whole 4x4x8 slice. The times are simulated.
256 devices in a mesh: row: 64 (over z, y, core), kk: 4 (over x).
Axes of the slice: x: 4, y: 4, z: 8, core: 2. Of those that a mesh axis runs over, the one named last changes fastest.
Arguments:
- left_blocks: bfloat16 [32768, 4096], P('row', 'kk'), may hold values from -6 to 6
- right_blocks: bfloat16 [4096, 8192], P('kk', 'row'), may hold values from -0.125 to 0.125
- left_mask: int32 [256, 32], P('row', 'kk'), may hold values 0 or 1
- right_mask: int32 [32, 64], P('kk', 'row'), may hold values 0 or 1
- out_mask: int32 [256, 64], P('row'), may hold values 0 or 1
Outputs:
- product_blocks: bfloat16 [32768, 8192], P(('row', 'kk'))
All inputs are finite; a program needn't handle non-finite values. No bound on the sum of `left_mask` or of `right_mask` or of `out_mask` on one device may be relied on, other than what follows from the above.
Results may differ from a plain program's by a relative error of at most 0.001.
Values may be sent and summed in bfloat16 or wider, within the bound.
No kernel may reach another device: no remote copies, remote signals or barrier semaphores. Data moves between devices by JAX's collectives and lax.ppermute only.
A program may use at most 192 MiB of HBM per device.

v0:
```python
import jax
import jax.numpy as jnp
from jax import lax
from jax.experimental import pallas as pl
from jax.experimental.pallas import tpu as pltpu
from jax.sharding import PartitionSpec as P


Z, Y, C, X = 8, 4, 2, 4
BS = 128
BOTH = ("row", "kk")


def flat(z, y, c, x):
    return ((z * Y + y) * C + c) * X + x


def move(v, source):
    pairs = []
    for z in range(Z):
        for y in range(Y):
            for c in range(C):
                for x in range(X):
                    sz, sy, sc, sx = source(z, y, c, x)
                    pairs.append((flat(sz % Z, sy % Y, sc, sx), flat(z, y, c, x)))
    return lax.ppermute(v, BOTH, pairs)


def from_y(v, d):
    return move(v, lambda z, y, c, x: (z, y + d, c, x))


def from_z(v, d):
    return move(v, lambda z, y, c, x: (z + d, y, c, x))


def from_share(v):
    return move(v, lambda z, y, c, x: (z, y, c, x ^ 1))


def from_reduce(v):
    return move(v, lambda z, y, c, x: (z, y, c, X - 1 - x))


def from_core(v):
    return move(v, lambda z, y, c, x: (z, y, 1 - c, x))


def spread(v):
    return [from_y(v, d) for d in range(1, Y)]


def mask_right(right, mask):
    depth, cols = right.shape
    blocks = mask.shape[1]

    def body(mask_ref, right_ref, out_ref):
        for k in range(blocks):
            rows = pl.ds(k * BS, BS)
            out_ref[rows, :] = right_ref[rows, :] * mask_ref[0, k].astype(jnp.float32).astype(jnp.bfloat16)

    return pl.pallas_call(
        body,
        out_shape=jax.ShapeDtypeStruct((depth, cols), jnp.bfloat16),
        in_specs=[pl.BlockSpec(memory_space=pltpu.SMEM), pl.BlockSpec(memory_space=pltpu.VMEM)],
        out_specs=pl.BlockSpec(memory_space=pltpu.VMEM),
        name="mask_right",
    )(mask, right)


def mask_left(left, mask, order):
    depth = left.shape[1]

    def body(order_ref, mask_ref, a_ref, b_ref, mine_ref, theirs_ref):
        i = pl.program_id(0)
        for src, dst, at in ((a_ref, mine_ref, order_ref[i]), (b_ref, theirs_ref, order_ref[i + 2])):
            for k in range(depth // BS):
                cols = pl.ds(k * BS, BS)
                dst[:, cols] = src[:, cols] * mask_ref[at, k].astype(jnp.float32).astype(jnp.bfloat16)

    out = jax.ShapeDtypeStruct((2 * BS, depth), jnp.bfloat16)
    return pl.pallas_call(
        body,
        out_shape=(out, out),
        grid_spec=pltpu.PrefetchScalarGridSpec(
            num_scalar_prefetch=2,
            grid=(2,),
            in_specs=[
                pl.BlockSpec((BS, depth), lambda i, o, m: (o[i], 0)),
                pl.BlockSpec((BS, depth), lambda i, o, m: (o[i + 2], 0)),
            ],
            out_specs=[pl.BlockSpec((BS, depth), lambda i, o, m: (i, 0))] * 2,
        ),
        name="mask_left",
    )(order, mask, left, left)


TAIL = 16


def code(v):
    return jnp.clip(jnp.floor(v + 0.5), -32767.0, 32767.0).astype(jnp.int32).astype(jnp.int16)


def value(q):
    return q.astype(jnp.int32).astype(jnp.float32)


def partial_product(lhs, steps):
    rows, depth2 = lhs.shape
    depth, quarter, width, count = depth2 // 2, rows // 4, 2 * BS, len(steps)
    arrays = []
    for step in steps:
        for a, _ in step:
            if not any(a is b for b in arrays):
                arrays.append(a)

    def which(a):
        return next(i for i, b in enumerate(arrays) if a is b)

    def body(lhs_ref, *refs):
        ins, (send_ref, keep_ref, right_ref, send_buf, keep_buf, in_sem, out_sem) = refs[: len(arrays)], refs[len(arrays) :]

        def load(src, i, j):
            dst = right_ref.at[i, pl.ds((j // 2) * depth, depth), pl.ds((j % 2) * BS, BS)]
            return pltpu.make_async_copy(src, dst, in_sem.at[i, j])

        for i, step in enumerate(steps):
            for j, (a, k) in enumerate(step):
                ref = ins[which(a)]
                load(ref if k is None else ref.at[k], i, j).start()

        def store(i):
            cols = pl.ds(pl.multiple_of(i * width, width), width)
            return (
                pltpu.make_async_copy(send_buf.at[i], send_ref.at[:, cols], out_sem.at[i, 0]),
                pltpu.make_async_copy(keep_buf.at[i], keep_ref.at[:, cols], out_sem.at[i, 1]),
            )

        def multiply(i, _):
            first, at = steps[0][0]
            for j in range(4):
                ref = ins[which(first)]
                load(ref if at is None else ref.at[at], i, j).wait()
            out = jnp.dot(lhs_ref[...], right_ref[i], preferred_element_type=jnp.float32)
            keep_buf[i, :quarter, :] = out[quarter : 2 * quarter]
            keep_buf[i, quarter:, :] = out[3 * quarter :]
            upper, lower = out[:quarter], out[2 * quarter : 3 * quarter]
            most = jnp.max(jnp.maximum(jnp.abs(upper), jnp.abs(lower)), axis=0, keepdims=True)
            exponent = jnp.ceil(jnp.log2(jnp.maximum(most, 1e-30)))
            scale = jnp.exp2(15.0 - exponent)
            send_buf[i, :quarter, :] = code(upper * scale)
            send_buf[i, quarter : 2 * quarter, :] = code(lower * scale)
            send_buf[i, 2 * quarter :, :] = code(jnp.broadcast_to(exponent, (TAIL, width)))
            for copy in store(i):
                copy.start()
            return 0

        lax.fori_loop(0, count, multiply, 0)
        for i in range(count):
            for copy in store(i):
                copy.wait()

    sent = jax.ShapeDtypeStruct((2 * quarter + TAIL, count * width), jnp.int16)
    kept = jax.ShapeDtypeStruct((2 * quarter, count * width), jnp.float32)
    anywhere = pl.BlockSpec(memory_space=pltpu.HBM)
    return pl.pallas_call(
        body,
        out_shape=(sent, kept),
        in_specs=[pl.BlockSpec(memory_space=pltpu.VMEM)] + [anywhere] * len(arrays),
        out_specs=(anywhere, anywhere),
        scratch_shapes=[
            pltpu.VMEM((count, depth2, width), jnp.bfloat16),
            pltpu.VMEM((count, 2 * quarter + TAIL, width), jnp.int16),
            pltpu.VMEM((count, 2 * quarter, width), jnp.float32),
            pltpu.SemaphoreType.DMA((count, 4)),
            pltpu.SemaphoreType.DMA((count, 2)),
        ],
        cost_estimate=pl.CostEstimate(
            flops=2 * rows * depth2 * count * width, bytes_accessed=(3 * count) << 19, transcendentals=0
        ),
        name="partial_product",
    )(lhs, *arrays)


def finish(parts):
    rows = parts[0][0].shape[0]
    half, count = rows // 2, len(parts)
    widths = [k.shape[1] for k, _ in parts]
    starts = [sum(widths[:i]) for i in range(count)]
    total = sum(widths)
    tall = 32

    def body(*refs):
        ins, (own_ref, other_ref, a_buf, b_buf, own_buf, other_buf, in_sem, out_sem) = refs[: 2 * count], refs[2 * count :]
        loads, stores = [], []
        for i in range(count):
            cols = pl.ds(starts[i], widths[i])
            loads.append(
                (
                    pltpu.make_async_copy(ins[2 * i], a_buf.at[:, cols], in_sem.at[i, 0]),
                    pltpu.make_async_copy(ins[2 * i + 1], b_buf.at[:, cols], in_sem.at[i, 1]),
                )
            )
            stores.append(
                (
                    pltpu.make_async_copy(own_buf.at[:, cols], own_ref.at[:, cols], out_sem.at[i, 0]),
                    pltpu.make_async_copy(other_buf.at[:, cols], other_ref.at[:, cols], out_sem.at[i, 1]),
                )
            )
        for pair in loads:
            for copy in pair:
                copy.start()
        for i in range(count):
            for copy in loads[i]:
                copy.wait()
            cols = pl.ds(starts[i], widths[i])
            unit = jnp.exp2(value(b_buf[rows:, cols])[:1] - 15.0)
            for base, dst in ((0, own_buf), (half, other_buf)):

                def add(r, _, base=base, dst=dst, cols=cols, unit=unit):
                    src = pl.ds(pl.multiple_of(base + r * tall, tall), tall)
                    to = pl.ds(pl.multiple_of(r * tall, tall), tall)
                    dst[to, cols] = (a_buf[src, cols] + value(b_buf[src, cols]) * unit).astype(jnp.bfloat16)
                    return 0

                lax.fori_loop(0, half // tall, add, 0)
            for copy in stores[i]:
                copy.start()
        for pair in stores:
            for copy in pair:
                copy.wait()

    out = jax.ShapeDtypeStruct((half, total), jnp.bfloat16)
    anywhere = pl.BlockSpec(memory_space=pltpu.HBM)
    return pl.pallas_call(
        body,
        out_shape=(out, out),
        in_specs=[anywhere] * (2 * count),
        out_specs=(anywhere, anywhere),
        scratch_shapes=[pltpu.VMEM((rows, total), jnp.float32), pltpu.VMEM((rows + TAIL, total), jnp.int16)]
        + [pltpu.VMEM((half, total), jnp.bfloat16)] * 2
        + [pltpu.SemaphoreType.DMA((count, 2))] * 2,
        cost_estimate=pl.CostEstimate(flops=rows * total * 2, bytes_accessed=rows * total * 10, transcendentals=0),
        name="finish",
    )(*(v for pair in parts for v in pair))


def place(out_mask, base, own, other, groups):
    rows = own[0].shape[0]
    count = len(groups)
    blocks = 4 * sum(len(steps) for steps in groups)

    def body(mask_ref, *refs):
        ends, (out_ref, buf, sem) = refs[-3 - 2 * count : -3], refs[-3:]
        z, y, c, x = position()
        copies = []
        for g, steps in enumerate(groups):
            for p, (d, h) in enumerate(steps):
                for k in range(2):
                    group = lax.rem(z + d % Z, Z) * Y + lax.rem(y + 2 * h + k, Y)
                    for src, core in ((ends[g], c), (ends[count + g], 1 - c)):
                        i, block = len(copies), group * C + core
                        scale = mask_ref[x, block].astype(jnp.float32).astype(jnp.bfloat16)
                        buf[i] = src[:, pl.ds((2 * p + k) * BS, BS)] * scale
                        cols = pl.ds(pl.multiple_of(block * BS, BS), BS)
                        copies.append(pltpu.make_async_copy(buf.at[i], out_ref.at[:, cols], sem.at[i]))
                        copies[-1].start()
        for copy in copies:
            copy.wait()

    smem, vmem, hbm = (pl.BlockSpec(memory_space=m) for m in (pltpu.SMEM, pltpu.VMEM, pltpu.HBM))
    bases = [] if base is None else [base]
    return pl.pallas_call(
        body,
        out_shape=jax.ShapeDtypeStruct((rows, Z * Y * C * BS), jnp.bfloat16),
        in_specs=[smem] + [hbm] * len(bases) + [vmem] * (2 * count),
        out_specs=hbm,
        input_output_aliases={1: 0} if bases else {},
        scratch_shapes=[pltpu.VMEM((blocks, rows, BS), jnp.bfloat16), pltpu.SemaphoreType.DMA((blocks,))],
        cost_estimate=pl.CostEstimate(flops=blocks * rows * BS, bytes_accessed=blocks * rows * BS * 4, transcendentals=0),
        name="place",
    )(out_mask, *bases, *own, *other)


def position():
    row, x = lax.axis_index("row"), lax.axis_index("kk")
    return row // (Y * C), (row // C) % Y, row % C, x


PAIRS = range(Y // 2)
SLOTS = {
    "0": [(0, h) for h in PAIRS],
    "4": [(4, h) for h in PAIRS],
    "1": [(d, h) for d in (1, -1) for h in PAIRS],
    "2": [(d, h) for d in (2, -2) for h in PAIRS],
    "3": [(d, h) for d in (3, -3) for h in PAIRS],
}
GROUPS = {"fin0": ("0", "1"), "fin1": ("2", "4"), "fin2": ("3",)}


def per_device(left_blocks, right_blocks, left_mask, right_mask, out_mask):
    x = lax.axis_index("kk")
    near = x + 1 - 2 * (x % 2)
    order = jnp.stack([X - 1 - x, x, X - 1 - near, near]).astype(jnp.int32)

    mine = mask_right(right_blocks, right_mask.T)
    theirs = from_share(mine)
    along = spread(mine)
    far = from_z(mine, 4)
    near_along = from_share(jnp.stack(along))
    own = {}
    line = {(0, 0): (theirs, None)}
    for k in range(1, Y):
        line[0, k] = (near_along, k - 1)

    hop = {}
    for s in (1, -1):
        first = from_z(theirs, s)
        line[s, 0] = (first, None)
        hop[s, 0] = jnp.stack([mine, *along, first])
        for d in (1, 2):
            packet = from_z(hop[s, d - 1], s)
            hop[s, d] = packet
            for k in range(Y):
                own[s * d, k] = (packet, k)
            line[s * (d + 1), 0] = (packet, Y)
        last = hop[s, 2][:Y]
        packet = from_z(last, s)
        for k in range(Y):
            own[s * 3, k] = (packet, k)
    for k in range(Y):
        own[0, k] = (hop[1, 0], k)

    def block(pair):
        array, index = pair
        return array if index is None else array[index]

    for d in (1, 2, 3):
        both = jnp.stack([block(line[d, 0]), block(line[-d, 0])])
        for k, got in enumerate(spread(both), 1):
            line[d, k], line[-d, k] = (got, 0), (got, 1)

    far_all = [far] + spread(far)
    near_far = from_share(jnp.stack(far_all))
    for k in range(Y):
        own[4, k], line[4, k] = (far_all[k], None), (near_far, k)

    own_rows, their_rows = mask_left(left_blocks, left_mask, order)
    half = jnp.concatenate([own_rows, from_share(their_rows)], axis=1)
    lhs = jnp.concatenate([half, from_core(half)], axis=0)

    sums = {}
    for slot, steps in SLOTS.items():
        send, keep = partial_product(
            lhs, [[table[d, 2 * h + k] for table in (own, line) for k in range(2)] for d, h in steps]
        )
        sums[slot] = (keep, from_reduce(send))
    own_ends, other_ends = [], []
    for slots in GROUPS.values():
        a, b = finish([sums[slot] for slot in slots])
        own_ends.append(a)
        other_ends.append(from_core(b))
    groups = [sum((SLOTS[slot] for slot in slots), []) for slots in GROUPS.values()]
    out = place(out_mask, None, own_ends[:-1], other_ends[:-1], groups[:-1])
    return place(out_mask, out, own_ends[-1:], other_ends[-1:], groups[-1:])


def solution(mesh):
    in_specs = (P("row", "kk"), P("kk", "row"), P("row", "kk"), P("kk", "row"), P("row", None))
    out_specs = P(("row", "kk"), None)

    return jax.shard_map(per_device, mesh=mesh, in_specs=in_specs, out_specs=out_specs, check_vma=False)
```

profile of v0, /device:TPU:1, one launch (start us, length us, event | category | flops | bytes accessed | tf_op | source)
XLA Modules:
  0.0 231.7 jit_solution(2643877227856960890)
XLA Ops:
  0.0 1.7 mask_right.1
  1.7 2.0 collective-permute-start.5
  3.7 2.7 %collective-permute-start.2 = (bf16[1024,128]{1,0:T(8,128)(2,1)}, bf16[1024,128]{1,0:T(8,128)(2,1)S(1)}, u32[]{:S(2)}, u32[]{:S(2)}) collective-permute-start(bf16[1024,128]{1,0:T(8,128)(2,1)} %mask_right.1), channel_id=1, source_target_pairs={{8,0},{9,1},{10,2},{11,3},{12,4},{13,5},{14,6},{15,7},{16,8},{17,9... | collective-permute-start | bytes 786440 | tf_op jit(solution)/shard_map/ppermute | solution.py:26
  7.5 1.0 bitcast_dynamic-update-slice_fusion.1
  8.8 6.7 %collective-permute-start.6 = (bf16[1024,128]{1,0:T(8,128)(2,1)S(1)}, bf16[1024,128]{1,0:T(8,128)(2,1)S(1)}, u32[]{:S(2)}, u32[]{:S(2)}) collective-permute-start(bf16[1024,128]{1,0:T(8,128)(2,1)S(1)} %collective-permute-done.5.refs_1_), channel_id=1, source_target_pairs={{32,0},{33,1},{34,2},{35,3},{36,4},{37,5},{38,6},{39,7},{40,8},{41... | collective-permute-start | bytes 786440 | tf_op jit(solution)/shard_map/ppermute | solution.py:26
  15.6 6.4 %collective-permute-done.4 = bf16[1024,128]{1,0:T(8,128)(2,1)S(1)} collective-permute-done((bf16[1024,128]{1,0:T(8,128)(2,1)}, bf16[1024,128]{1,0:T(8,128)(2,1)S(1)}, u32[]{:S(2)}, u32[]{:S(2)}) %collective-permute-start.4) | collective-permute-done | bytes 262176 | tf_op jit(solution)/shard_map/ppermute | solution.py:26
  23.0 5.7 %collective-permute-start.9 = (bf16[5,1024,128]{2,1,0:T(8,128)(2,1)S(1)}, bf16[5,1024,128]{2,1,0:T(8,128)(2,1)}, u32[]{:S(2)}, u32[]{:S(2)}) collective-permute-start(bf16[5,1024,128]{2,1,0:T(8,128)(2,1)S(1)} %constant_dynamic-update-slice_fusion.2.refs_0_), channel_id=1, source_target_pairs={{32,0},{33,1},{34,2},{35,3},{36,4},{37,5},{38,6},{39,7},{40,8},{41... | collective-permute-start | bytes 3932168 | tf_op jit(solution)/shard_map/ppermute | solution.py:26
  29.4 2.9 %mask_left.1 = (bf16[256,1024]{1,0:T(8,128)(2,1)}, bf16[256,1024]{1,0:T(8,128)(2,1)}) custom-call(s32[4]{0:T(128)} %pad_add_fusion.order_ref, s32[4,8]{1,0:T(4,128)} %mask_ref.3, bf16[512,1024]{1,0:T(8,128)(2,1)} %b_ref.1, bf16[512,1024]{1,0:T(8,128)(2,1)} %b_ref.1), custom_call_target="tpu_custom_call" | custom-call | tf_op jit(solution)/shard_map/mask_left/pallas_call | solution.py:82
  32.5 2.8 %collective-permute-start.22 = (bf16[1024,128]{1,0:T(8,128)(2,1)S(1)}, bf16[1024,128]{1,0:T(8,128)(2,1)S(1)}, u32[]{:S(2)}, u32[]{:S(2)}) collective-permute-start(bf16[1024,128]{1,0:T(8,128)(2,1)S(1)} %copy-done.3), channel_id=1, source_target_pairs={{128,0},{129,1},{130,2},{131,3},{132,4},{133,5},{134,6},{135,7},{1... | collective-permute-start | bytes 786440 | tf_op jit(solution)/shard_map/ppermute | solution.py:26
  35.3 31.8 %collective-permute-done.9.refs_0_.refs_1_ = bf16[5,1024,128]{2,1,0:T(8,128)(2,1)} collective-permute-done((bf16[5,1024,128]{2,1,0:T(8,128)(2,1)S(1)}, bf16[5,1024,128]{2,1,0:T(8,128)(2,1)}, u32[]{:S(2)}, u32[]{:S(2)}) %collective-permute-start.9) | collective-permute-done | bytes 1310752 | tf_op jit(solution)/shard_map/ppermute | solution.py:26
  67.1 3.8 %collective-permute-start.16 = (bf16[5,1024,128]{2,1,0:T(8,128)(2,1)}, bf16[5,1024,128]{2,1,0:T(8,128)(2,1)S(1)}, u32[]{:S(2)}, u32[]{:S(2)}) collective-permute-start(bf16[5,1024,128]{2,1,0:T(8,128)(2,1)} %collective-permute-done.9.refs_0_.refs_1_), channel_id=1, source_target_pairs={{32,0},{33,1},{34,2},{35,3},{36,4},{37,5},{38,6},{39,7},{40,8},{41... | collective-permute-start | bytes 3932168 | tf_op jit(solution)/shard_map/ppermute | solution.py:26
  70.9 1.5 collective-permute-start.25
  72.4 1.1 constant_dynamic-update-slice_fusion.1
  74.0 2.4 %collective-permute-done.23.refs_1_ = bf16[1024,128]{1,0:T(8,128)(2,1)S(1)} collective-permute-done((bf16[1024,128]{1,0:T(8,128)(2,1)S(1)}, bf16[1024,128]{1,0:T(8,128)(2,1)S(1)}, u32[]{:S(2)}, u32[]{:S(2)}) %collective-permute-start.23) | collective-permute-done | bytes 262176 | tf_op jit(solution)/shard_map/ppermute | solution.py:26
  76.4 1.2 collective-permute-start.11
  77.8 9.5 %collective-permute-start.1 = (bf16[256,2048]{1,0:T(8,128)(2,1)S(1)}, bf16[256,2048]{1,0:T(8,128)(2,1)S(1)}, u32[]{:S(2)}, u32[]{:S(2)}) collective-permute-start(bf16[256,2048]{1,0:T(8,128)(2,1)S(1)} %constant_dynamic-update-slice_fusion), channel_id=1, source_target_pairs={{4,0},{5,1},{6,2},{7,3},{0,4},{1,5},{2,6},{3,7},{12,8},{13,9},{14,... | collective-permute-start | bytes 3145736 | tf_op jit(solution)/shard_map/ppermute | solution.py:26
  87.2 6.2 %collective-permute-done.11.refs_2_ = bf16[2,1024,128]{2,1,0:T(8,128)(2,1)S(1)} collective-permute-done((bf16[2,1024,128]{2,1,0:T(8,128)(2,1)S(1)}, bf16[2,1024,128]{2,1,0:T(8,128)(2,1)S(1)}, u32[]{:S(2)}, u32[]{:S(2)}) %collective-permute-start.11) | collective-permute-done | bytes 524320 | tf_op jit(solution)/shard_map/ppermute | solution.py:26
  93.8 1.0 slice.25
  94.8 1.0 slice.24
  95.8 6.3 %collective-permute-done.12.refs_3_ = bf16[2,1024,128]{2,1,0:T(8,128)(2,1)S(1)} collective-permute-done((bf16[2,1024,128]{2,1,0:T(8,128)(2,1)S(1)}, bf16[2,1024,128]{2,1,0:T(8,128)(2,1)S(1)}, u32[]{:S(2)}, u32[]{:S(2)}) %collective-permute-start.12) | collective-permute-done | bytes 524320 | tf_op jit(solution)/shard_map/ppermute | solution.py:26
  102.2 4.9 %collective-permute-start.17 = (bf16[2,1024,128]{2,1,0:T(8,128)(2,1)S(1)}, bf16[2,1024,128]{2,1,0:T(8,128)(2,1)S(1)}, u32[]{:S(2)}, u32[]{:S(2)}) collective-permute-start(bf16[2,1024,128]{2,1,0:T(8,128)(2,1)S(1)} %pad_maximum_fusion.4), channel_id=1, source_target_pairs={{8,0},{9,1},{10,2},{11,3},{12,4},{13,5},{14,6},{15,7},{16,8},{17,9... | collective-permute-start | bytes 1572872 | tf_op jit(solution)/shard_map/ppermute | solution.py:26
  107.2 1.3 collective-permute-start.19
  109.5 3.0 %collective-permute-done.13.refs_4_ = bf16[2,1024,128]{2,1,0:T(8,128)(2,1)S(1)} collective-permute-done((bf16[2,1024,128]{2,1,0:T(8,128)(2,1)S(1)}, bf16[2,1024,128]{2,1,0:T(8,128)(2,1)S(1)}, u32[]{:S(2)}, u32[]{:S(2)}) %collective-permute-start.13) | collective-permute-done | bytes 524320 | tf_op jit(solution)/shard_map/ppermute | solution.py:26
  113.0 2.8 %collective-permute-done.17.refs_2_ = bf16[2,1024,128]{2,1,0:T(8,128)(2,1)S(1)} collective-permute-done((bf16[2,1024,128]{2,1,0:T(8,128)(2,1)S(1)}, bf16[2,1024,128]{2,1,0:T(8,128)(2,1)S(1)}, u32[]{:S(2)}, u32[]{:S(2)}) %collective-permute-start.17) | collective-permute-done | bytes 524320 | tf_op jit(solution)/shard_map/ppermute | solution.py:26
  116.6 3.6 %collective-permute-start.30 = (bf16[4,1024,128]{2,1,0:T(8,128)(2,1)S(1)}, bf16[4,1024,128]{2,1,0:T(8,128)(2,1)}, u32[]{:S(2)}, u32[]{:S(2)}) collective-permute-start(bf16[4,1024,128]{2,1,0:T(8,128)(2,1)S(1)} %slice.26), channel_id=1, source_target_pairs={{32,0},{33,1},{34,2},{35,3},{36,4},{37,5},{38,6},{39,7},{40,8},{41... | collective-permute-start | bytes 3145736 | tf_op jit(solution)/shard_map/ppermute | solution.py:26
  120.3 1.4 collective-permute-done.18.refs_3_
  121.9 14.9 %collective-permute-done.19.refs_4_ = bf16[2,1024,128]{2,1,0:T(8,128)(2,1)S(1)} collective-permute-done((bf16[2,1024,128]{2,1,0:T(8,128)(2,1)S(1)}, bf16[2,1024,128]{2,1,0:T(8,128)(2,1)S(1)}, u32[]{:S(2)}, u32[]{:S(2)}) %collective-permute-start.19) | collective-permute-done | bytes 524320 | tf_op jit(solution)/shard_map/ppermute | solution.py:26
  137.1 1.0 pad_maximum_fusion.2
  138.4 1.0 collective-permute-start.7
  139.4 4.9 %collective-permute-done.32.refs_3_ = bf16[2,1024,128]{2,1,0:T(8,128)(2,1)} collective-permute-done((bf16[2,1024,128]{2,1,0:T(8,128)(2,1)}, bf16[2,1024,128]{2,1,0:T(8,128)(2,1)}, u32[]{:S(2)}, u32[]{:S(2)}) %collective-permute-start.32) | collective-permute-done | bytes 524320 | tf_op jit(solution)/shard_map/ppermute | solution.py:26
  144.3 4.7 %collective-permute-start.33 = (bf16[2,1024,128]{2,1,0:T(8,128)(2,1)}, bf16[2,1024,128]{2,1,0:T(8,128)(2,1)}, u32[]{:S(2)}, u32[]{:S(2)}) collective-permute-start(bf16[2,1024,128]{2,1,0:T(8,128)(2,1)} %pad_maximum_fusion.5), channel_id=1, source_target_pairs={{24,0},{25,1},{26,2},{27,3},{28,4},{29,5},{30,6},{31,7},{0,8},{1,9... | collective-permute-start | bytes 1572872 | tf_op jit(solution)/shard_map/ppermute | solution.py:26
  149.0 1.6 pad_maximum_fusion.lhs_ref
  150.5 6.9 %partial_product.6 = (s16[272,1024]{1,0:T(8,128)(2,1)}, f32[256,1024]{1,0:T(8,128)}) custom-call(bf16[512,2048]{1,0:T(8,128)(2,1)} %pad_maximum_fusion.lhs_ref, bf16[5,1024,128]{2,1,0:T(8,128)(2,1)} %collective-permute-done.9.refs_0_.refs_1_, bf16[1024,128]{1,0:T(8,128)(2,1)} %copy-done.4, bf16[2,1024,128]{2,1,0:T(8,128)(2,1)} %copy-done.27, ...), custom_call_target="tpu_custom_call" | custom-call | flops 2147483648 | bytes 6291456 | tf_op jit(solution)/shard_map/partial_product/pallas_call | solution.py:167
  157.4 6.9 %partial_product.7 = (s16[272,1024]{1,0:T(8,128)(2,1)}, f32[256,1024]{1,0:T(8,128)}) custom-call(bf16[512,2048]{1,0:T(8,128)(2,1)} %pad_maximum_fusion.lhs_ref, bf16[5,1024,128]{2,1,0:T(8,128)(2,1)} %copy-done, bf16[5,1024,128]{2,1,0:T(8,128)(2,1)} %collective-permute-done.9.refs_0_.refs_1_, bf16[2,1024,128]{2,1,0:T(8,128)(2,1)} %copy-done.18, ...), custom_call_target="tpu_custom_call" | custom-call | flops 2147483648 | bytes 6291456 | tf_op jit(solution)/shard_map/partial_product/pallas_call | solution.py:167
  164.4 1.9 collective-permute-start.15
  167.2 6.9 %partial_product.9 = (s16[272,1024]{1,0:T(8,128)(2,1)}, f32[256,1024]{1,0:T(8,128)}) custom-call(bf16[512,2048]{1,0:T(8,128)(2,1)} %pad_maximum_fusion.lhs_ref, bf16[4,1024,128]{2,1,0:T(8,128)(2,1)} %collective-permute-done.30.refs_0_, bf16[5,1024,128]{2,1,0:T(8,128)(2,1)} %copy-done, bf16[2,1024,128]{2,1,0:T(8,128)(2,1)} %collective-permute-done.31.refs_2_, ...), custom_call_target="tpu_custom_call" | custom-call | flops 2147483648 | bytes 6291456 | tf_op jit(solution)/shard_map/partial_product/pallas_call | solution.py:167
  174.0 1.9 collective-permute-start.35
  176.0 5.2 %partial_product.5 = (s16[272,512]{1,0:T(8,128)(2,1)}, f32[256,512]{1,0:T(8,128)}) custom-call(bf16[512,2048]{1,0:T(8,128)(2,1)} %pad_maximum_fusion.lhs_ref, bf16[5,1024,128]{2,1,0:T(8,128)(2,1)} %copy-done.2, bf16[1024,128]{1,0:T(8,128)(2,1)} %copy-done.25, bf16[3,1024,128]{2,1,0:T(8,128)(2,1)} %collective-permute-done.7.refs_2_), custom_call_target="tpu_custom_call" | custom-call | flops 1073741824 | bytes 3145728 | tf_op jit(solution)/shard_map/partial_product/pallas_call | solution.py:167
  181.2 1.1 collective-permute-start.8
  182.2 5.2 %partial_product.8 = (s16[272,512]{1,0:T(8,128)(2,1)}, f32[256,512]{1,0:T(8,128)}) custom-call(bf16[512,2048]{1,0:T(8,128)(2,1)} %pad_maximum_fusion.lhs_ref, bf16[1024,128]{1,0:T(8,128)(2,1)} %copy-done.12, bf16[1024,128]{1,0:T(8,128)(2,1)} %copy-done.13, bf16[4,1024,128]{2,1,0:T(8,128)(2,1)} %collective-permute-done.26.refs_2_, ...), custom_call_target="tpu_custom_call" | custom-call | flops 1073741824 | bytes 3145728 | tf_op jit(solution)/shard_map/partial_product/pallas_call | solution.py:167
  187.5 1.8 collective-permute-start.27
  189.3 15.0 %collective-permute-done.8.refs_1_ = s16[272,512]{1,0:T(8,128)(2,1)S(1)} collective-permute-done((s16[272,512]{1,0:T(8,128)(2,1)}, s16[272,512]{1,0:T(8,128)(2,1)S(1)}, u32[]{:S(2)}, u32[]{:S(2)}) %collective-permute-start.8) | collective-permute-done | bytes 278560 | tf_op jit(solution)/shard_map/ppermute | solution.py:26
  204.9 2.7 %finish.3 = (bf16[128,1536]{1,0:T(8,128)(2,1)}, bf16[128,1536]{1,0:T(8,128)(2,1)}) custom-call(f32[256,512]{1,0:T(8,128)} %get-tuple-element.25.refs_0_, s16[272,512]{1,0:T(8,128)(2,1)} %copy-done.24, f32[256,1024]{1,0:T(8,128)} %get-tuple-element.27.refs_2_, s16[272,1024]{1,0:T(8,128)(2,1)} %collective-permute-done.15.refs_3_), custom_call_target="tpu_custom_call" | custom-call | flops 786432 | bytes 3932160 | tf_op jit(solution)/shard_map/finish/pallas_call | solution.py:236
  207.7 9.6 %collective-permute-start.28 = (bf16[128,1536]{1,0:T(8,128)(2,1)}, bf16[128,1536]{1,0:T(8,128)(2,1)S(1)}, u32[]{:S(2)}, u32[]{:S(2)}) collective-permute-start(bf16[128,1536]{1,0:T(8,128)(2,1)} %get-tuple-element.35), channel_id=1, source_target_pairs={{4,0},{5,1},{6,2},{7,3},{0,4},{1,5},{2,6},{3,7},{12,8},{13,9},{14,... | collective-permute-start | bytes 1179656 | tf_op jit(solution)/shard_map/ppermute | solution.py:26
  218.2 2.5 %finish.4 = (bf16[128,1536]{1,0:T(8,128)(2,1)}, bf16[128,1536]{1,0:T(8,128)(2,1)}) custom-call(f32[256,1024]{1,0:T(8,128)} %get-tuple-element.30.refs_0_, s16[272,1024]{1,0:T(8,128)(2,1)} %copy-done.16, f32[256,512]{1,0:T(8,128)} %get-tuple-element.32.refs_2_, s16[272,512]{1,0:T(8,128)(2,1)} %copy-done.23), custom_call_target="tpu_custom_call" | custom-call | flops 786432 | bytes 3932160 | tf_op jit(solution)/shard_map/finish/pallas_call | solution.py:236
  221.6 2.4 %finish.5 = (bf16[128,1024]{1,0:T(8,128)(2,1)}, bf16[128,1024]{1,0:T(8,128)(2,1)}) custom-call(f32[256,1024]{1,0:T(8,128)} %get-tuple-element.37.refs_0_, s16[272,1024]{1,0:T(8,128)(2,1)} %copy-done.17), custom_call_target="tpu_custom_call" | custom-call | flops 524288 | bytes 2621440 | tf_op jit(solution)/shard_map/finish/pallas_call | solution.py:236
  225.5 3.3 %place.2.refs_0_ = bf16[128,8192]{1,0:T(8,128)(2,1)} custom-call(s32[4,64]{1,0:T(4,128)} %mask_ref.5, bf16[128,1536]{1,0:T(8,128)(2,1)} %get-tuple-element.29.refs_0_, bf16[128,1536]{1,0:T(8,128)(2,1)} %get-tuple-element.34.refs_1_, bf16[128,1536]{1,0:T(8,128)(2,1)} %copy-done.21, bf16[128,1536]{1,0:T(8,128)(2,1)} %copy-done.22), custom_call_target="tpu_custom_call" | custom-call | flops 786432 | bytes 3145728 | tf_op jit(solution)/shard_map/place/pallas_call | solution.py:274
  229.5 2.1 place.3
  (120 shorter events, 13.2 us)
Async XLA Ops:
  1.7 7.1 %collective-permute-start.5 = (bf16[1024,128]{1,0:T(8,128)(2,1)}, bf16[1024,128]{1,0:T(8,128)(2,1)S(1)}, u32[]{:S(2)}, u32[]{:S(2)}) collective-permute-start(bf16[1024,128]{1,0:T(8,128)(2,1)} %mask_right.1), channel_id=1, source_target_pairs={{1,0},{0,1},{3,2},{2,3},{5,4},{4,5},{7,6},{6,7},{9,8},{8,9},{11,10... | collective-permute-start | bytes 786440 | tf_op jit(solution)/shard_map/ppermute | solution.py:26
  3.7 11.8 %collective-permute-start.2 = (bf16[1024,128]{1,0:T(8,128)(2,1)}, bf16[1024,128]{1,0:T(8,128)(2,1)S(1)}, u32[]{:S(2)}, u32[]{:S(2)}) collective-permute-start(bf16[1024,128]{1,0:T(8,128)(2,1)} %mask_right.1), channel_id=1, source_target_pairs={{8,0},{9,1},{10,2},{11,3},{12,4},{13,5},{14,6},{15,7},{16,8},{17,9... | collective-permute-start | bytes 786440 | tf_op jit(solution)/shard_map/ppermute | solution.py:26
  6.5 9.1 %collective-permute-start.3 = (bf16[1024,128]{1,0:T(8,128)(2,1)}, bf16[1024,128]{1,0:T(8,128)(2,1)S(1)}, u32[]{:S(2)}, u32[]{:S(2)}) collective-permute-start(bf16[1024,128]{1,0:T(8,128)(2,1)} %mask_right.1), channel_id=1, source_target_pairs={{16,0},{17,1},{18,2},{19,3},{20,4},{21,5},{22,6},{23,7},{24,8},{25... | collective-permute-start | bytes 786440 | tf_op jit(solution)/shard_map/ppermute | solution.py:26
  6.8 15.2 %collective-permute-start.4 = (bf16[1024,128]{1,0:T(8,128)(2,1)}, bf16[1024,128]{1,0:T(8,128)(2,1)S(1)}, u32[]{:S(2)}, u32[]{:S(2)}) collective-permute-start(bf16[1024,128]{1,0:T(8,128)(2,1)} %mask_right.1), channel_id=1, source_target_pairs={{24,0},{25,1},{26,2},{27,3},{28,4},{29,5},{30,6},{31,7},{0,8},{1,9... | collective-permute-start | bytes 786440 | tf_op jit(solution)/shard_map/ppermute | solution.py:26
  8.8 14.1 %collective-permute-start.6 = (bf16[1024,128]{1,0:T(8,128)(2,1)S(1)}, bf16[1024,128]{1,0:T(8,128)(2,1)S(1)}, u32[]{:S(2)}, u32[]{:S(2)}) collective-permute-start(bf16[1024,128]{1,0:T(8,128)(2,1)S(1)} %collective-permute-done.5.refs_1_), channel_id=1, source_target_pairs={{32,0},{33,1},{34,2},{35,3},{36,4},{37,5},{38,6},{39,7},{40,8},{41... | collective-permute-start | bytes 786440 | tf_op jit(solution)/shard_map/ppermute | solution.py:26
  15.5 13.1 %collective-permute-start.10 = (bf16[1024,128]{1,0:T(8,128)(2,1)S(1)}, bf16[1024,128]{1,0:T(8,128)(2,1)S(1)}, u32[]{:S(2)}, u32[]{:S(2)}) collective-permute-start(bf16[1024,128]{1,0:T(8,128)(2,1)S(1)} %collective-permute-done.5.refs_1_), channel_id=1, source_target_pairs={{224,0},{225,1},{226,2},{227,3},{228,4},{229,5},{230,6},{231,7},{2... | collective-permute-start | bytes 786440 | tf_op jit(solution)/shard_map/ppermute | solution.py:26
  22.9 50.6 %copy-start.4 = (bf16[1024,128]{1,0:T(8,128)(2,1)}, bf16[1024,128]{1,0:T(8,128)(2,1)S(1)}, u32[]{:S(2)}) copy-start(bf16[1024,128]{1,0:T(8,128)(2,1)S(1)} %collective-permute-done.6.refs_1_) | copy-start | bytes 786436
  23.0 44.1 %collective-permute-start.9 = (bf16[5,1024,128]{2,1,0:T(8,128)(2,1)S(1)}, bf16[5,1024,128]{2,1,0:T(8,128)(2,1)}, u32[]{:S(2)}, u32[]{:S(2)}) collective-permute-start(bf16[5,1024,128]{2,1,0:T(8,128)(2,1)S(1)} %constant_dynamic-update-slice_fusion.2.refs_0_), channel_id=1, source_target_pairs={{32,0},{33,1},{34,2},{35,3},{36,4},{37,5},{38,6},{39,7},{40,8},{41... | collective-permute-start | bytes 3932168 | tf_op jit(solution)/shard_map/ppermute | solution.py:26
  28.6 44.8 %copy-start.5 = (bf16[1024,128]{1,0:T(8,128)(2,1)}, bf16[1024,128]{1,0:T(8,128)(2,1)S(1)}, u32[]{:S(2)}) copy-start(bf16[1024,128]{1,0:T(8,128)(2,1)S(1)} %collective-permute-done.10.refs_6_) | copy-start | bytes 786436
  28.7 42.1 %collective-permute-start.14 = (bf16[5,1024,128]{2,1,0:T(8,128)(2,1)S(1)}, bf16[5,1024,128]{2,1,0:T(8,128)(2,1)}, u32[]{:S(2)}, u32[]{:S(2)}) collective-permute-start(bf16[5,1024,128]{2,1,0:T(8,128)(2,1)S(1)} %constant_dynamic-update-slice_fusion.6), channel_id=1, source_target_pairs={{224,0},{225,1},{226,2},{227,3},{228,4},{229,5},{230,6},{231,7},{2... | collective-permute-start | bytes 3932168 | tf_op jit(solution)/shard_map/ppermute | solution.py:26
  32.3 41.3 %collective-permute-start = (bf16[256,1024]{1,0:T(8,128)(2,1)}, bf16[256,1024]{1,0:T(8,128)(2,1)S(1)}, u32[]{:S(2)}, u32[]{:S(2)}) collective-permute-start(bf16[256,1024]{1,0:T(8,128)(2,1)} %get-tuple-element.24), channel_id=1, source_target_pairs={{1,0},{0,1},{3,2},{2,3},{5,4},{4,5},{7,6},{6,7},{9,8},{8,9},{11,10... | collective-permute-start | bytes 1572872 | tf_op jit(solution)/shard_map/ppermute | solution.py:26
  32.5 38.4 %collective-permute-start.22 = (bf16[1024,128]{1,0:T(8,128)(2,1)S(1)}, bf16[1024,128]{1,0:T(8,128)(2,1)S(1)}, u32[]{:S(2)}, u32[]{:S(2)}) collective-permute-start(bf16[1024,128]{1,0:T(8,128)(2,1)S(1)} %copy-done.3), channel_id=1, source_target_pairs={{128,0},{129,1},{130,2},{131,3},{132,4},{133,5},{134,6},{135,7},{1... | collective-permute-start | bytes 786440 | tf_op jit(solution)/shard_map/ppermute | solution.py:26
  67.1 40.1 %collective-permute-start.16 = (bf16[5,1024,128]{2,1,0:T(8,128)(2,1)}, bf16[5,1024,128]{2,1,0:T(8,128)(2,1)S(1)}, u32[]{:S(2)}, u32[]{:S(2)}) collective-permute-start(bf16[5,1024,128]{2,1,0:T(8,128)(2,1)} %collective-permute-done.9.refs_0_.refs_1_), channel_id=1, source_target_pairs={{32,0},{33,1},{34,2},{35,3},{36,4},{37,5},{38,6},{39,7},{40,8},{41... | collective-permute-start | bytes 3932168 | tf_op jit(solution)/shard_map/ppermute | solution.py:26
  70.8 36.4 %collective-permute-start.20 = (bf16[5,1024,128]{2,1,0:T(8,128)(2,1)}, bf16[5,1024,128]{2,1,0:T(8,128)(2,1)S(1)}, u32[]{:S(2)}, u32[]{:S(2)}) collective-permute-start(bf16[5,1024,128]{2,1,0:T(8,128)(2,1)} %collective-permute-done.14.refs_5_.refs_6_), channel_id=1, source_target_pairs={{224,0},{225,1},{226,2},{227,3},{228,4},{229,5},{230,6},{231,7},{2... | collective-permute-start | bytes 3932168 | tf_op jit(solution)/shard_map/ppermute | solution.py:26
  70.9 50.9 %copy-start.12 = (bf16[1024,128]{1,0:T(8,128)(2,1)}, bf16[1024,128]{1,0:T(8,128)(2,1)S(1)}, u32[]{:S(2)}) copy-start(bf16[1024,128]{1,0:T(8,128)(2,1)S(1)} %collective-permute-done.22.refs_0_) | copy-start | bytes 786436
  70.9 5.6 %collective-permute-start.23 = (bf16[1024,128]{1,0:T(8,128)(2,1)S(1)}, bf16[1024,128]{1,0:T(8,128)(2,1)S(1)}, u32[]{:S(2)}, u32[]{:S(2)}) collective-permute-start(bf16[1024,128]{1,0:T(8,128)(2,1)S(1)} %collective-permute-done.22.refs_0_), channel_id=1, source_target_pairs={{8,0},{9,1},{10,2},{11,3},{12,4},{13,5},{14,6},{15,7},{16,8},{17,9... | collective-permute-start | bytes 786440 | tf_op jit(solution)/shard_map/ppermute | solution.py:26
  70.9 6.8 %collective-permute-start.25 = (bf16[1024,128]{1,0:T(8,128)(2,1)S(1)}, bf16[1024,128]{1,0:T(8,128)(2,1)S(1)}, u32[]{:S(2)}, u32[]{:S(2)}) collective-permute-start(bf16[1024,128]{1,0:T(8,128)(2,1)S(1)} %collective-permute-done.22.refs_0_), channel_id=1, source_target_pairs={{24,0},{25,1},{26,2},{27,3},{28,4},{29,5},{30,6},{31,7},{0,8},{1,9... | collective-permute-start | bytes 786440 | tf_op jit(solution)/shard_map/ppermute | solution.py:26
  73.6 13.7 %collective-permute-start.24 = (bf16[1024,128]{1,0:T(8,128)(2,1)S(1)}, bf16[1024,128]{1,0:T(8,128)(2,1)S(1)}, u32[]{:S(2)}, u32[]{:S(2)}) collective-permute-start(bf16[1024,128]{1,0:T(8,128)(2,1)S(1)} %collective-permute-done.22.refs_0_), channel_id=1, source_target_pairs={{16,0},{17,1},{18,2},{19,3},{20,4},{21,5},{22,6},{23,7},{24,8},{25... | collective-permute-start | bytes 786440 | tf_op jit(solution)/shard_map/ppermute | solution.py:26
  76.4 45.3 %copy-start.13 = (bf16[1024,128]{1,0:T(8,128)(2,1)}, bf16[1024,128]{1,0:T(8,128)(2,1)S(1)}, u32[]{:S(2)}) copy-start(bf16[1024,128]{1,0:T(8,128)(2,1)S(1)} %collective-permute-done.23.refs_1_) | copy-start | bytes 786436
  76.4 17.0 %collective-permute-start.11 = (bf16[2,1024,128]{2,1,0:T(8,128)(2,1)S(1)}, bf16[2,1024,128]{2,1,0:T(8,128)(2,1)S(1)}, u32[]{:S(2)}, u32[]{:S(2)}) collective-permute-start(bf16[2,1024,128]{2,1,0:T(8,128)(2,1)S(1)} %pad_maximum_fusion.3), channel_id=1, source_target_pairs={{8,0},{9,1},{10,2},{11,3},{12,4},{13,5},{14,6},{15,7},{16,8},{17,9... | collective-permute-start | bytes 1572872 | tf_op jit(solution)/shard_map/ppermute | solution.py:26
  77.7 44.0 %copy-start.14 = (bf16[1024,128]{1,0:T(8,128)(2,1)}, bf16[1024,128]{1,0:T(8,128)(2,1)S(1)}, u32[]{:S(2)}) copy-start(bf16[1024,128]{1,0:T(8,128)(2,1)S(1)} %collective-permute-done.25.refs_4_) | copy-start | bytes 786436
  77.8 35.2 %collective-permute-start.1 = (bf16[256,2048]{1,0:T(8,128)(2,1)S(1)}, bf16[256,2048]{1,0:T(8,128)(2,1)S(1)}, u32[]{:S(2)}, u32[]{:S(2)}) collective-permute-start(bf16[256,2048]{1,0:T(8,128)(2,1)S(1)} %constant_dynamic-update-slice_fusion), channel_id=1, source_target_pairs={{4,0},{5,1},{6,2},{7,3},{0,4},{1,5},{2,6},{3,7},{12,8},{13,9},{14,... | collective-permute-start | bytes 3145736 | tf_op jit(solution)/shard_map/ppermute | solution.py:26
  87.2 34.6 %copy-start.15 = (bf16[1024,128]{1,0:T(8,128)(2,1)}, bf16[1024,128]{1,0:T(8,128)(2,1)S(1)}, u32[]{:S(2)}) copy-start(bf16[1024,128]{1,0:T(8,128)(2,1)S(1)} %collective-permute-done.24.refs_3_) | copy-start | bytes 786436
  87.2 14.9 %collective-permute-start.12 = (bf16[2,1024,128]{2,1,0:T(8,128)(2,1)S(1)}, bf16[2,1024,128]{2,1,0:T(8,128)(2,1)S(1)}, u32[]{:S(2)}, u32[]{:S(2)}) collective-permute-start(bf16[2,1024,128]{2,1,0:T(8,128)(2,1)S(1)} %pad_maximum_fusion.3), channel_id=1, source_target_pairs={{16,0},{17,1},{18,2},{19,3},{20,4},{21,5},{22,6},{23,7},{24,8},{25... | collective-permute-start | bytes 1572872 | tf_op jit(solution)/shard_map/ppermute | solution.py:26
  93.5 15.1 %copy-start.27 = (bf16[2,1024,128]{2,1,0:T(8,128)(2,1)}, bf16[2,1024,128]{2,1,0:T(8,128)(2,1)S(1)}, u32[]{:S(2)}) copy-start(bf16[2,1024,128]{2,1,0:T(8,128)(2,1)S(1)} %collective-permute-done.11.refs_2_) | copy-start | bytes 1572868
  93.5 18.9 %collective-permute-start.13 = (bf16[2,1024,128]{2,1,0:T(8,128)(2,1)S(1)}, bf16[2,1024,128]{2,1,0:T(8,128)(2,1)S(1)}, u32[]{:S(2)}, u32[]{:S(2)}) collective-permute-start(bf16[2,1024,128]{2,1,0:T(8,128)(2,1)S(1)} %pad_maximum_fusion.3), channel_id=1, source_target_pairs={{24,0},{25,1},{26,2},{27,3},{28,4},{29,5},{30,6},{31,7},{0,8},{1,9... | collective-permute-start | bytes 1572872 | tf_op jit(solution)/shard_map/ppermute | solution.py:26
  102.2 13.6 %collective-permute-start.17 = (bf16[2,1024,128]{2,1,0:T(8,128)(2,1)S(1)}, bf16[2,1024,128]{2,1,0:T(8,128)(2,1)S(1)}, u32[]{:S(2)}, u32[]{:S(2)}) collective-permute-start(bf16[2,1024,128]{2,1,0:T(8,128)(2,1)S(1)} %pad_maximum_fusion.4), channel_id=1, source_target_pairs={{8,0},{9,1},{10,2},{11,3},{12,4},{13,5},{14,6},{15,7},{16,8},{17,9... | collective-permute-start | bytes 1572872 | tf_op jit(solution)/shard_map/ppermute | solution.py:26
  107.1 14.6 %collective-permute-start.18 = (bf16[2,1024,128]{2,1,0:T(8,128)(2,1)S(1)}, bf16[2,1024,128]{2,1,0:T(8,128)(2,1)S(1)}, u32[]{:S(2)}, u32[]{:S(2)}) collective-permute-start(bf16[2,1024,128]{2,1,0:T(8,128)(2,1)S(1)} %pad_maximum_fusion.4), channel_id=1, source_target_pairs={{16,0},{17,1},{18,2},{19,3},{20,4},{21,5},{22,6},{23,7},{24,8},{25... | collective-permute-start | bytes 1572872 | tf_op jit(solution)/shard_map/ppermute | solution.py:26
  107.2 29.6 %collective-permute-start.19 = (bf16[2,1024,128]{2,1,0:T(8,128)(2,1)S(1)}, bf16[2,1024,128]{2,1,0:T(8,128)(2,1)S(1)}, u32[]{:S(2)}, u32[]{:S(2)}) collective-permute-start(bf16[2,1024,128]{2,1,0:T(8,128)(2,1)S(1)} %pad_maximum_fusion.4), channel_id=1, source_target_pairs={{24,0},{25,1},{26,2},{27,3},{28,4},{29,5},{30,6},{31,7},{0,8},{1,9... | collective-permute-start | bytes 1572872 | tf_op jit(solution)/shard_map/ppermute | solution.py:26
  112.4 26.0 %collective-permute-start.31 = (bf16[2,1024,128]{2,1,0:T(8,128)(2,1)}, bf16[2,1024,128]{2,1,0:T(8,128)(2,1)}, u32[]{:S(2)}, u32[]{:S(2)}) collective-permute-start(bf16[2,1024,128]{2,1,0:T(8,128)(2,1)} %pad_maximum_fusion.5), channel_id=1, source_target_pairs={{8,0},{9,1},{10,2},{11,3},{12,4},{13,5},{14,6},{15,7},{16,8},{17,9... | collective-permute-start | bytes 1572872 | tf_op jit(solution)/shard_map/ppermute | solution.py:26
  112.9 31.4 %collective-permute-start.32 = (bf16[2,1024,128]{2,1,0:T(8,128)(2,1)}, bf16[2,1024,128]{2,1,0:T(8,128)(2,1)}, u32[]{:S(2)}, u32[]{:S(2)}) collective-permute-start(bf16[2,1024,128]{2,1,0:T(8,128)(2,1)} %pad_maximum_fusion.5), channel_id=1, source_target_pairs={{16,0},{17,1},{18,2},{19,3},{20,4},{21,5},{22,6},{23,7},{24,8},{25... | collective-permute-start | bytes 1572872 | tf_op jit(solution)/shard_map/ppermute | solution.py:26
  116.6 49.7 %collective-permute-start.30 = (bf16[4,1024,128]{2,1,0:T(8,128)(2,1)S(1)}, bf16[4,1024,128]{2,1,0:T(8,128)(2,1)}, u32[]{:S(2)}, u32[]{:S(2)}) collective-permute-start(bf16[4,1024,128]{2,1,0:T(8,128)(2,1)S(1)} %slice.26), channel_id=1, source_target_pairs={{32,0},{33,1},{34,2},{35,3},{36,4},{37,5},{38,6},{39,7},{40,8},{41... | collective-permute-start | bytes 3145736 | tf_op jit(solution)/shard_map/ppermute | solution.py:26
  120.3 16.8 %copy-start.7 = (bf16[1024,128]{1,0:T(8,128)(2,1)S(1)}, bf16[1024,128]{1,0:T(8,128)(2,1)}, u32[]{:S(2)}) copy-start(bf16[1024,128]{1,0:T(8,128)(2,1)} %copy-done.6) | copy-start | bytes 786436
  120.3 16.8 %copy-start.9 = (bf16[1024,128]{1,0:T(8,128)(2,1)S(1)}, bf16[1024,128]{1,0:T(8,128)(2,1)}, u32[]{:S(2)}) copy-start(bf16[1024,128]{1,0:T(8,128)(2,1)} %copy-done.8) | copy-start | bytes 786436
  120.3 16.8 %copy-start.11 = (bf16[1024,128]{1,0:T(8,128)(2,1)S(1)}, bf16[1024,128]{1,0:T(8,128)(2,1)}, u32[]{:S(2)}) copy-start(bf16[1024,128]{1,0:T(8,128)(2,1)} %copy-done.10) | copy-start | bytes 786436
  121.7 16.3 %copy-start.19 = (bf16[2,1024,128]{2,1,0:T(8,128)(2,1)}, bf16[2,1024,128]{2,1,0:T(8,128)(2,1)S(1)}, u32[]{:S(2)}) copy-start(bf16[2,1024,128]{2,1,0:T(8,128)(2,1)S(1)} %collective-permute-done.18.refs_3_) | copy-start | bytes 1572868
  121.7 45.4 %collective-permute-start.34 = (bf16[4,1024,128]{2,1,0:T(8,128)(2,1)S(1)}, bf16[4,1024,128]{2,1,0:T(8,128)(2,1)}, u32[]{:S(2)}, u32[]{:S(2)}) collective-permute-start(bf16[4,1024,128]{2,1,0:T(8,128)(2,1)S(1)} %slice.29), channel_id=1, source_target_pairs={{224,0},{225,1},{226,2},{227,3},{228,4},{229,5},{230,6},{231,7},{2... | collective-permute-start | bytes 3145736 | tf_op jit(solution)/shard_map/ppermute | solution.py:26
  136.8 45.4 %collective-permute-start.26 = (bf16[4,1024,128]{2,1,0:T(8,128)(2,1)S(1)}, bf16[4,1024,128]{2,1,0:T(8,128)(2,1)}, u32[]{:S(2)}, u32[]{:S(2)}) collective-permute-start(bf16[4,1024,128]{2,1,0:T(8,128)(2,1)S(1)} %pad_maximum_fusion.1), channel_id=1, source_target_pairs={{1,0},{0,1},{3,2},{2,3},{5,4},{4,5},{7,6},{6,7},{9,8},{8,9},{11,10... | collective-permute-start | bytes 3145736 | tf_op jit(solution)/shard_map/ppermute | solution.py:26
  138.4 37.5 %collective-permute-start.7 = (bf16[3,1024,128]{2,1,0:T(8,128)(2,1)}, bf16[3,1024,128]{2,1,0:T(8,128)(2,1)}, u32[]{:S(2)}, u32[]{:S(2)}) collective-permute-start(bf16[3,1024,128]{2,1,0:T(8,128)(2,1)} %pad_maximum_fusion.2), channel_id=1, source_target_pairs={{1,0},{0,1},{3,2},{2,3},{5,4},{4,5},{7,6},{6,7},{9,8},{8,9},{11,10... | collective-permute-start | bytes 2359304 | tf_op jit(solution)/shard_map/ppermute | solution.py:26
  144.3 20.1 %collective-permute-start.33 = (bf16[2,1024,128]{2,1,0:T(8,128)(2,1)}, bf16[2,1024,128]{2,1,0:T(8,128)(2,1)}, u32[]{:S(2)}, u32[]{:S(2)}) collective-permute-start(bf16[2,1024,128]{2,1,0:T(8,128)(2,1)} %pad_maximum_fusion.5), channel_id=1, source_target_pairs={{24,0},{25,1},{26,2},{27,3},{28,4},{29,5},{30,6},{31,7},{0,8},{1,9... | collective-permute-start | bytes 1572872 | tf_op jit(solution)/shard_map/ppermute | solution.py:26
  164.4 39.9 %collective-permute-start.15 = (s16[272,1024]{1,0:T(8,128)(2,1)}, s16[272,1024]{1,0:T(8,128)(2,1)}, u32[]{:S(2)}, u32[]{:S(2)}) collective-permute-start(s16[272,1024]{1,0:T(8,128)(2,1)} %get-tuple-element.28), channel_id=1, source_target_pairs={{3,0},{2,1},{1,2},{0,3},{7,4},{6,5},{5,6},{4,7},{11,8},{10,9},{9,1... | collective-permute-start | bytes 1671176 | tf_op jit(solution)/shard_map/ppermute | solution.py:26
  166.3 51.0 %collective-permute-start.21 = (s16[272,1024]{1,0:T(8,128)(2,1)}, s16[272,1024]{1,0:T(8,128)(2,1)S(1)}, u32[]{:S(2)}, u32[]{:S(2)}) collective-permute-start(s16[272,1024]{1,0:T(8,128)(2,1)} %get-tuple-element.31), channel_id=1, source_target_pairs={{3,0},{2,1},{1,2},{0,3},{7,4},{6,5},{5,6},{4,7},{11,8},{10,9},{9,1... | collective-permute-start | bytes 1671176 | tf_op jit(solution)/shard_map/ppermute | solution.py:26
  174.0 46.8 %collective-permute-start.35 = (s16[272,1024]{1,0:T(8,128)(2,1)}, s16[272,1024]{1,0:T(8,128)(2,1)S(1)}, u32[]{:S(2)}, u32[]{:S(2)}) collective-permute-start(s16[272,1024]{1,0:T(8,128)(2,1)} %get-tuple-element.38), channel_id=1, source_target_pairs={{3,0},{2,1},{1,2},{0,3},{7,4},{6,5},{5,6},{4,7},{11,8},{10,9},{9,1... | collective-permute-start | bytes 1671176 | tf_op jit(solution)/shard_map/ppermute | solution.py:26
  181.2 23.1 %collective-permute-start.8 = (s16[272,512]{1,0:T(8,128)(2,1)}, s16[272,512]{1,0:T(8,128)(2,1)S(1)}, u32[]{:S(2)}, u32[]{:S(2)}) collective-permute-start(s16[272,512]{1,0:T(8,128)(2,1)} %get-tuple-element.26), channel_id=1, source_target_pairs={{3,0},{2,1},{1,2},{0,3},{7,4},{6,5},{5,6},{4,7},{11,8},{10,9},{9,1... | collective-permute-start | bytes 835592 | tf_op jit(solution)/shard_map/ppermute | solution.py:26
  187.5 29.8 %collective-permute-start.27 = (s16[272,512]{1,0:T(8,128)(2,1)}, s16[272,512]{1,0:T(8,128)(2,1)S(1)}, u32[]{:S(2)}, u32[]{:S(2)}) collective-permute-start(s16[272,512]{1,0:T(8,128)(2,1)} %get-tuple-element.33), channel_id=1, source_target_pairs={{3,0},{2,1},{1,2},{0,3},{7,4},{6,5},{5,6},{4,7},{11,8},{10,9},{9,1... | collective-permute-start | bytes 835592 | tf_op jit(solution)/shard_map/ppermute | solution.py:26
  207.7 16.9 %collective-permute-start.28 = (bf16[128,1536]{1,0:T(8,128)(2,1)}, bf16[128,1536]{1,0:T(8,128)(2,1)S(1)}, u32[]{:S(2)}, u32[]{:S(2)}) collective-permute-start(bf16[128,1536]{1,0:T(8,128)(2,1)} %get-tuple-element.35), channel_id=1, source_target_pairs={{4,0},{5,1},{6,2},{7,3},{0,4},{1,5},{2,6},{3,7},{12,8},{13,9},{14,... | collective-permute-start | bytes 1179656 | tf_op jit(solution)/shard_map/ppermute | solution.py:26
  220.7 3.9 %collective-permute-start.29 = (bf16[128,1536]{1,0:T(8,128)(2,1)}, bf16[128,1536]{1,0:T(8,128)(2,1)S(1)}, u32[]{:S(2)}, u32[]{:S(2)}) collective-permute-start(bf16[128,1536]{1,0:T(8,128)(2,1)} %get-tuple-element.36), channel_id=1, source_target_pairs={{4,0},{5,1},{6,2},{7,3},{0,4},{1,5},{2,6},{3,7},{12,8},{13,9},{14,... | collective-permute-start | bytes 1179656 | tf_op jit(solution)/shard_map/ppermute | solution.py:26
  224.0 4.7 %collective-permute-start.36 = (bf16[128,1024]{1,0:T(8,128)(2,1)}, bf16[128,1024]{1,0:T(8,128)(2,1)S(1)}, u32[]{:S(2)}, u32[]{:S(2)}) collective-permute-start(bf16[128,1024]{1,0:T(8,128)(2,1)} %get-tuple-element.40), channel_id=1, source_target_pairs={{4,0},{5,1},{6,2},{7,3},{0,4},{1,5},{2,6},{3,7},{12,8},{13,9},{14,... | collective-permute-start | bytes 786440 | tf_op jit(solution)/shard_map/ppermute | solution.py:26
  (19 other events, 81.7 us)
where the time goes:
time: 233 us; the launch traced here: 232 us
  waiting for transfers between devices  95.9 us (41%)
  starting transfers between devices  72.2 us (31%)
  Pallas kernels  48.6 us (21%)
  local copies, waits for them, and re-layouts  10.1 us (4%)
  other arithmetic  4.23 us (2%)
    ppermute x37, waiting for transfers between devices, move(): return lax.ppermute(v, BOTH, pairs)  95.9 us
    ppermute x37, starting transfers between devices, move(): return lax.ppermute(v, BOTH, pairs)  72.2 us
    pallas_call x5, Pallas kernels, partial_product(): pl.pallas_call(body, out_shape=(sent, kept), in_specs=[pl.BlockSpec(memor...  31.1 us
    unnamed x66, local copies, waits for them, and re-layouts  7.85 us
    pallas_call x3, Pallas kernels, finish(): pl.pallas_call(body, out_shape=(out, out), in_specs=[anywhere] * (2 * cou...  7.61 us
    pallas_call x2, Pallas kernels, place(): pl.pallas_call(body, out_shape=jax.ShapeDtypeStruct((rows, Z * Y * C * BS...  5.31 us
  transfers between devices with their start and end apart: 37, of which 14 were waited for; matrix products, arithmetic and copies ran while one was open for 4% of the time, Pallas kernels for 19%

commit v1 on v0

--- a/solution.py
+++ b/solution.py
@@ -1,3 +1,5 @@
+import functools
+
 import jax
 import jax.numpy as jnp
 from jax import lax
@@ -64,6 +66,7 @@
         out_shape=jax.ShapeDtypeStruct((depth, cols), jnp.bfloat16),
         in_specs=[pl.BlockSpec(memory_space=pltpu.SMEM), pl.BlockSpec(memory_space=pltpu.VMEM)],
         out_specs=pl.BlockSpec(memory_space=pltpu.VMEM),
+        compiler_params=pltpu.CompilerParams(vmem_limit_bytes=8 << 20),
         name="mask_right",
     )(mask, right)
 
@@ -91,6 +94,7 @@
             ],
             out_specs=[pl.BlockSpec((BS, depth), lambda i, o, m: (i, 0))] * 2,
         ),
+        compiler_params=pltpu.CompilerParams(vmem_limit_bytes=8 << 20),
         name="mask_left",
     )(order, mask, left, left)
 
@@ -119,63 +123,42 @@
         return next(i for i, b in enumerate(arrays) if a is b)
 
     def body(lhs_ref, *refs):
-        ins, (send_ref, keep_ref, right_ref, send_buf, keep_buf, in_sem, out_sem) = refs[: len(arrays)], refs[len(arrays) :]
-
-        def load(src, i, j):
-            dst = right_ref.at[i, pl.ds((j // 2) * depth, depth), pl.ds((j % 2) * BS, BS)]
-            return pltpu.make_async_copy(src, dst, in_sem.at[i, j])
-
-        for i, step in enumerate(steps):
+        ins, (send_ref, keep_ref, right_ref) = refs[: len(arrays)], refs[len(arrays) :]
+
+        def fill(step):
             for j, (a, k) in enumerate(step):
                 ref = ins[which(a)]
-                load(ref if k is None else ref.at[k], i, j).start()
-
-        def store(i):
+                block = ref[...] if k is None else ref[k]
+                right_ref[pl.ds((j // 2) * depth, depth), pl.ds((j % 2) * BS, BS)] = block
+
+        def multiply(i, _):
+            for k, step in enumerate(steps):
+                pl.when(i == k)(functools.partial(fill, step))
+            out = jnp.dot(lhs_ref[...], right_ref[...], preferred_element_type=jnp.float32)
             cols = pl.ds(pl.multiple_of(i * width, width), width)
-            return (
-                pltpu.make_async_copy(send_buf.at[i], send_ref.at[:, cols], out_sem.at[i, 0]),
-                pltpu.make_async_copy(keep_buf.at[i], keep_ref.at[:, cols], out_sem.at[i, 1]),
-            )
-
-        def multiply(i, _):
-            first, at = steps[0][0]
-            for j in range(4):
-                ref = ins[which(first)]
-                load(ref if at is None else ref.at[at], i, j).wait()
-            out = jnp.dot(lhs_ref[...], right_ref[i], preferred_element_type=jnp.float32)
-            keep_buf[i, :quarter, :] = out[quarter : 2 * quarter]
-            keep_buf[i, quarter:, :] = out[3 * quarter :]
+            keep_ref[:quarter, cols] = out[quarter : 2 * quarter]
+            keep_ref[quarter:, cols] = out[3 * quarter :]
             upper, lower = out[:quarter], out[2 * quarter : 3 * quarter]
             most = jnp.max(jnp.maximum(jnp.abs(upper), jnp.abs(lower)), axis=0, keepdims=True)
             exponent = jnp.ceil(jnp.log2(jnp.maximum(most, 1e-30)))
             scale = jnp.exp2(15.0 - exponent)
-            send_buf[i, :quarter, :] = code(upper * scale)
-            send_buf[i, quarter : 2 * quarter, :] = code(lower * scale)
-            send_buf[i, 2 * quarter :, :] = code(jnp.broadcast_to(exponent, (TAIL, width)))
-            for copy in store(i):
-                copy.start()
+            send_ref[:quarter, cols] = code(upper * scale)
+            send_ref[quarter : 2 * quarter, cols] = code(lower * scale)
+            send_ref[2 * quarter :, cols] = code(jnp.broadcast_to(exponent, (TAIL, width)))
             return 0
 
         lax.fori_loop(0, count, multiply, 0)
-        for i in range(count):
-            for copy in store(i):
-                copy.wait()
 
     sent = jax.ShapeDtypeStruct((2 * quarter + TAIL, count * width), jnp.int16)
     kept = jax.ShapeDtypeStruct((2 * quarter, count * width), jnp.float32)
-    anywhere = pl.BlockSpec(memory_space=pltpu.HBM)
+    vmem = pl.BlockSpec(memory_space=pltpu.VMEM)
     return pl.pallas_call(
         body,
         out_shape=(sent, kept),
-        in_specs=[pl.BlockSpec(memory_space=pltpu.VMEM)] + [anywhere] * len(arrays),
-        out_specs=(anywhere, anywhere),
-        scratch_shapes=[
-            pltpu.VMEM((count, depth2, width), jnp.bfloat16),
-            pltpu.VMEM((count, 2 * quarter + TAIL, width), jnp.int16),
-            pltpu.VMEM((count, 2 * quarter, width), jnp.float32),
-            pltpu.SemaphoreType.DMA((count, 4)),
-            pltpu.SemaphoreType.DMA((count, 2)),
-        ],
+        in_specs=[vmem] * (1 + len(arrays)),
+        out_specs=(vmem, vmem),
+        scratch_shapes=[pltpu.VMEM((depth2, width), jnp.bfloat16)],
+        compiler_params=pltpu.CompilerParams(vmem_limit_bytes=24 << 20),
         cost_estimate=pl.CostEstimate(
             flops=2 * rows * depth2 * count * width, bytes_accessed=(3 * count) << 19, transcendentals=0
         ),
@@ -192,55 +175,29 @@
     tall = 32
 
     def body(*refs):
-        ins, (own_ref, other_ref, a_buf, b_buf, own_buf, other_buf, in_sem, out_sem) = refs[: 2 * count], refs[2 * count :]
-        loads, stores = [], []
+        ins, ends = refs[: 2 * count], refs[2 * count :]
         for i in range(count):
+            kept_ref, got_ref = ins[2 * i : 2 * i + 2]
             cols = pl.ds(starts[i], widths[i])
-            loads.append(
-                (
-                    pltpu.make_async_copy(ins[2 * i], a_buf.at[:, cols], in_sem.at[i, 0]),
-                    pltpu.make_async_copy(ins[2 * i + 1], b_buf.at[:, cols], in_sem.at[i, 1]),
-                )
-            )
-            stores.append(
-                (
-                    pltpu.make_async_copy(own_buf.at[:, cols], own_ref.at[:, cols], out_sem.at[i, 0]),
-                    pltpu.make_async_copy(other_buf.at[:, cols], other_ref.at[:, cols], out_sem.at[i, 1]),
-                )
-            )
-        for pair in loads:
-            for copy in pair:
-                copy.start()
-        for i in range(count):
-            for copy in loads[i]:
-                copy.wait()
-            cols = pl.ds(starts[i], widths[i])
-            unit = jnp.exp2(value(b_buf[rows:, cols])[:1] - 15.0)
-            for base, dst in ((0, own_buf), (half, other_buf)):
-
-                def add(r, _, base=base, dst=dst, cols=cols, unit=unit):
+            unit = jnp.exp2(value(got_ref[rows:, :])[:1] - 15.0)
+            for base, dst in zip((0, half), ends):
+
+                def add(r, _, base=base, dst=dst, cols=cols, unit=unit, kept_ref=kept_ref, got_ref=got_ref):
                     src = pl.ds(pl.multiple_of(base + r * tall, tall), tall)
                     to = pl.ds(pl.multiple_of(r * tall, tall), tall)
-                    dst[to, cols] = (a_buf[src, cols] + value(b_buf[src, cols]) * unit).astype(jnp.bfloat16)
+                    dst[to, cols] = (kept_ref[src, :] + value(got_ref[src, :]) * unit).astype(jnp.bfloat16)
                     return 0
 
                 lax.fori_loop(0, half // tall, add, 0)
-            for copy in stores[i]:
-                copy.start()
-        for pair in stores:
-            for copy in pair:
-                copy.wait()
 
     out = jax.ShapeDtypeStruct((half, total), jnp.bfloat16)
-    anywhere = pl.BlockSpec(memory_space=pltpu.HBM)
+    vmem = pl.BlockSpec(memory_space=pltpu.VMEM)
     return pl.pallas_call(
         body,
         out_shape=(out, out),
-        in_specs=[anywhere] * (2 * count),
-        out_specs=(anywhere, anywhere),
-        scratch_shapes=[pltpu.VMEM((rows, total), jnp.float32), pltpu.VMEM((rows + TAIL, total), jnp.int16)]
-        + [pltpu.VMEM((half, total), jnp.bfloat16)] * 2
-        + [pltpu.SemaphoreType.DMA((count, 2))] * 2,
+        in_specs=[vmem] * (2 * count),
+        out_specs=(vmem, vmem),
+        compiler_params=pltpu.CompilerParams(vmem_limit_bytes=12 << 20),
         cost_estimate=pl.CostEstimate(flops=rows * total * 2, bytes_accessed=rows * total * 10, transcendentals=0),
         name="finish",
     )(*(v for pair in parts for v in pair))
@@ -278,6 +235,7 @@
         out_specs=hbm,
         input_output_aliases={1: 0} if bases else {},
         scratch_shapes=[pltpu.VMEM((blocks, rows, BS), jnp.bfloat16), pltpu.SemaphoreType.DMA((blocks,))],
+        compiler_params=pltpu.CompilerParams(vmem_limit_bytes=12 << 20),
         cost_estimate=pl.CostEstimate(flops=blocks * rows * BS, bytes_accessed=blocks * rows * BS * 4, transcendentals=0),
         name="place",
     )(out_mask, *bases, *own, *other)

time: 233 us -> 221 us (0.948)
  waiting for transfers between devices: 95.9 us -> 120 us
  Pallas kernels: 48.6 us -> 25.1 us
  starting transfers between devices: 72.2 us -> 67.7 us
  local copies, waits for them, and re-layouts: 10.1 us -> 6.47 us
  other arithmetic: 4.23 us -> 0.69 us
    ppermute x37, waiting for transfers between devices: 95.9 us -> 120 us  [move(): return lax.ppermute(v, BOTH, pairs)]
    pallas_call x8, Pallas kernels: 38.7 us -> 19.5 us  [the longest x5 18.6 us: partial_product(): pl.pallas_call(body, out_shape=(sent, kept), in_specs=[vmem] * (1 + len(a...]
    ppermute x37, starting transfers between devices: 72.2 us -> 67.7 us  [move(): return lax.ppermute(v, BOTH, pairs)]
    unnamed x66 -> x28, local copies, waits for them, and re-layouts: 7.85 us -> 3.57 us
  transfers between devices with their start and end apart: 37 -> 37, of which waited for: 14 -> 17; matrix products, arithmetic and copies ran while one was open for 4% -> 2% of each run, Pallas kernels for 19% -> 10%
where the time goes in v1:
time: 221 us; the launch traced here: 220 us
  waiting for transfers between devices  120 us (54%)
  starting transfers between devices  67.7 us (31%)
  Pallas kernels  25.1 us (11%)
  local copies, waits for them, and re-layouts  6.47 us (3%)
    ppermute x37, waiting for transfers between devices, move(): return lax.ppermute(v, BOTH, pairs)  120 us
    ppermute x37, starting transfers between devices, move(): return lax.ppermute(v, BOTH, pairs)  67.7 us
    pallas_call x5, Pallas kernels, partial_product(): pl.pallas_call(body, out_shape=(sent, kept), in_specs=[vmem] * (1 + len(a...  18.6 us
  transfers between devices with their start and end apart: 37, of which 17 were waited for; matrix products, arithmetic and copies ran while one was open for 2% of the time, Pallas kernels for 10%

profile of v1, /device:TPU:1, one launch (start us, length us, event | category | flops | bytes accessed | tf_op | source)
XLA Modules:
  0.0 220.1 jit_solution(17795268382979838013)
XLA Ops:
  0.0 0.9 copy-done.1
  2.2 2.1 collective-permute-start.5
  4.3 2.7 %collective-permute-start.2 = (bf16[1024,128]{1,0:T(8,128)(2,1)S(1)}, bf16[1024,128]{1,0:T(8,128)(2,1)S(1)}, u32[]{:S(2)}, u32[]{:S(2)}) collective-permute-start(bf16[1024,128]{1,0:T(8,128)(2,1)S(1)} %mask_right.1), channel_id=1, source_target_pairs={{8,0},{9,1},{10,2},{11,3},{12,4},{13,5},{14,6},{15,7},{16,8},{17,9... | collective-permute-start | bytes 786440 | tf_op jit(solution)/shard_map/ppermute | solution.py:28
  8.1 1.0 collective-permute-done.5.refs_1_
  9.1 6.8 %collective-permute-start.6 = (bf16[1024,128]{1,0:T(8,128)(2,1)S(1)}, bf16[1024,128]{1,0:T(8,128)(2,1)S(1)}, u32[]{:S(2)}, u32[]{:S(2)}) collective-permute-start(bf16[1024,128]{1,0:T(8,128)(2,1)S(1)} %collective-permute-done.5.refs_1_), channel_id=1, source_target_pairs={{32,0},{33,1},{34,2},{35,3},{36,4},{37,5},{38,6},{39,7},{40,8},{41... | collective-permute-start | bytes 786440 | tf_op jit(solution)/shard_map/ppermute | solution.py:28
  16.0 6.4 %collective-permute-done.4 = bf16[1024,128]{1,0:T(8,128)(2,1)S(1)} collective-permute-done((bf16[1024,128]{1,0:T(8,128)(2,1)S(1)}, bf16[1024,128]{1,0:T(8,128)(2,1)S(1)}, u32[]{:S(2)}, u32[]{:S(2)}) %collective-permute-start.4) | collective-permute-done | bytes 262176 | tf_op jit(solution)/shard_map/ppermute | solution.py:28
  23.2 1.1 copy.12
  24.3 5.7 %collective-permute-start.9 = (bf16[5,1024,128]{2,1,0:T(8,128)(2,1)S(1)}, bf16[5,1024,128]{2,1,0:T(8,128)(2,1)}, u32[]{:S(2)}, u32[]{:S(2)}) collective-permute-start(bf16[5,1024,128]{2,1,0:T(8,128)(2,1)S(1)} %constant_dynamic-update-slice_fusion.2.refs_0_), channel_id=1, source_target_pairs={{32,0},{33,1},{34,2},{35,3},{36,4},{37,5},{38,6},{39,7},{40,8},{41... | collective-permute-start | bytes 3932168 | tf_op jit(solution)/shard_map/ppermute | solution.py:28
  30.7 0.9 mask_left.1
  32.0 2.8 %collective-permute-start.22 = (bf16[1024,128]{1,0:T(8,128)(2,1)S(1)}, bf16[1024,128]{1,0:T(8,128)(2,1)S(1)}, u32[]{:S(2)}, u32[]{:S(2)}) collective-permute-start(bf16[1024,128]{1,0:T(8,128)(2,1)S(1)} %mask_right.1), channel_id=1, source_target_pairs={{128,0},{129,1},{130,2},{131,3},{132,4},{133,5},{134,6},{135,7},{1... | collective-permute-start | bytes 786440 | tf_op jit(solution)/shard_map/ppermute | solution.py:28
  34.8 33.6 %collective-permute-done.9.refs_0_.refs_1_ = bf16[5,1024,128]{2,1,0:T(8,128)(2,1)} collective-permute-done((bf16[5,1024,128]{2,1,0:T(8,128)(2,1)S(1)}, bf16[5,1024,128]{2,1,0:T(8,128)(2,1)}, u32[]{:S(2)}, u32[]{:S(2)}) %collective-permute-start.9) | collective-permute-done | bytes 1310752 | tf_op jit(solution)/shard_map/ppermute | solution.py:28
  68.3 3.8 %collective-permute-start.16 = (bf16[5,1024,128]{2,1,0:T(8,128)(2,1)}, bf16[5,1024,128]{2,1,0:T(8,128)(2,1)S(1)}, u32[]{:S(2)}, u32[]{:S(2)}) collective-permute-start(bf16[5,1024,128]{2,1,0:T(8,128)(2,1)} %collective-permute-done.9.refs_0_.refs_1_), channel_id=1, source_target_pairs={{32,0},{33,1},{34,2},{35,3},{36,4},{37,5},{38,6},{39,7},{40,8},{41... | collective-permute-start | bytes 3932168 | tf_op jit(solution)/shard_map/ppermute | solution.py:28
  72.1 0.9 collective-permute-done.22.refs_0_
  73.0 1.5 collective-permute-start.25
  75.0 3.5 %collective-permute-done.23.refs_1_ = bf16[1024,128]{1,0:T(8,128)(2,1)S(1)} collective-permute-done((bf16[1024,128]{1,0:T(8,128)(2,1)S(1)}, bf16[1024,128]{1,0:T(8,128)(2,1)S(1)}, u32[]{:S(2)}, u32[]{:S(2)}) %collective-permute-start.23) | collective-permute-done | bytes 262176 | tf_op jit(solution)/shard_map/ppermute | solution.py:28
  78.5 1.2 collective-permute-start.11
  79.8 1.9 collective-permute-done.25.refs_4_
  81.7 7.9 %collective-permute-start.1 = (bf16[256,2048]{1,0:T(8,128)(2,1)S(1)}, bf16[256,2048]{1,0:T(8,128)(2,1)S(1)}, u32[]{:S(2)}, u32[]{:S(2)}) collective-permute-start(bf16[256,2048]{1,0:T(8,128)(2,1)S(1)} %constant_dynamic-update-slice_fusion), channel_id=1, source_target_pairs={{4,0},{5,1},{6,2},{7,3},{0,4},{1,5},{2,6},{3,7},{12,8},{13,9},{14,... | collective-permute-start | bytes 3145736 | tf_op jit(solution)/shard_map/ppermute | solution.py:28
  89.6 5.2 %collective-permute-done.11.refs_2_ = bf16[2,1024,128]{2,1,0:T(8,128)(2,1)S(1)} collective-permute-done((bf16[2,1024,128]{2,1,0:T(8,128)(2,1)S(1)}, bf16[2,1024,128]{2,1,0:T(8,128)(2,1)S(1)}, u32[]{:S(2)}, u32[]{:S(2)}) %collective-permute-start.11) | collective-permute-done | bytes 524320 | tf_op jit(solution)/shard_map/ppermute | solution.py:28
  94.9 1.0 slice.25
  95.9 1.0 slice.24
  96.9 7.6 %collective-permute-done.12.refs_3_ = bf16[2,1024,128]{2,1,0:T(8,128)(2,1)S(1)} collective-permute-done((bf16[2,1024,128]{2,1,0:T(8,128)(2,1)S(1)}, bf16[2,1024,128]{2,1,0:T(8,128)(2,1)S(1)}, u32[]{:S(2)}, u32[]{:S(2)}) %collective-permute-start.12) | collective-permute-done | bytes 524320 | tf_op jit(solution)/shard_map/ppermute | solution.py:28
  104.6 3.9 %collective-permute-start.17 = (bf16[2,1024,128]{2,1,0:T(8,128)(2,1)S(1)}, bf16[2,1024,128]{2,1,0:T(8,128)(2,1)S(1)}, u32[]{:S(2)}, u32[]{:S(2)}) collective-permute-start(bf16[2,1024,128]{2,1,0:T(8,128)(2,1)S(1)} %pad_maximum_fusion.4), channel_id=1, source_target_pairs={{8,0},{9,1},{10,2},{11,3},{12,4},{13,5},{14,6},{15,7},{16,8},{17,9... | collective-permute-start | bytes 1572872 | tf_op jit(solution)/shard_map/ppermute | solution.py:28
  109.2 6.4 %collective-permute-done.13.refs_4_ = bf16[2,1024,128]{2,1,0:T(8,128)(2,1)S(1)} collective-permute-done((bf16[2,1024,128]{2,1,0:T(8,128)(2,1)S(1)}, bf16[2,1024,128]{2,1,0:T(8,128)(2,1)S(1)}, u32[]{:S(2)}, u32[]{:S(2)}) %collective-permute-start.13) | collective-permute-done | bytes 524320 | tf_op jit(solution)/shard_map/ppermute | solution.py:28
  115.7 1.8 collective-permute-done.17.refs_2_
  117.4 2.8 %collective-permute-start.30 = (bf16[4,1024,128]{2,1,0:T(8,128)(2,1)S(1)}, bf16[4,1024,128]{2,1,0:T(8,128)(2,1)S(1)}, u32[]{:S(2)}, u32[]{:S(2)}) collective-permute-start(bf16[4,1024,128]{2,1,0:T(8,128)(2,1)S(1)} %slice.26), channel_id=1, source_target_pairs={{32,0},{33,1},{34,2},{35,3},{36,4},{37,5},{38,6},{39,7},{40,8},{41... | collective-permute-start | bytes 3145736 | tf_op jit(solution)/shard_map/ppermute | solution.py:28
  120.3 4.4 %collective-permute-done.18.refs_3_ = bf16[2,1024,128]{2,1,0:T(8,128)(2,1)S(1)} collective-permute-done((bf16[2,1024,128]{2,1,0:T(8,128)(2,1)S(1)}, bf16[2,1024,128]{2,1,0:T(8,128)(2,1)S(1)}, u32[]{:S(2)}, u32[]{:S(2)}) %collective-permute-start.18) | collective-permute-done | bytes 524320 | tf_op jit(solution)/shard_map/ppermute | solution.py:28
  124.9 14.3 %collective-permute-done.19.refs_4_ = bf16[2,1024,128]{2,1,0:T(8,128)(2,1)S(1)} collective-permute-done((bf16[2,1024,128]{2,1,0:T(8,128)(2,1)S(1)}, bf16[2,1024,128]{2,1,0:T(8,128)(2,1)S(1)}, u32[]{:S(2)}, u32[]{:S(2)}) %collective-permute-start.19) | collective-permute-done | bytes 524320 | tf_op jit(solution)/shard_map/ppermute | solution.py:28
  139.9 1.0 collective-permute-start.7
  140.9 6.3 %collective-permute-done.32.refs_3_ = bf16[2,1024,128]{2,1,0:T(8,128)(2,1)S(1)} collective-permute-done((bf16[2,1024,128]{2,1,0:T(8,128)(2,1)S(1)}, bf16[2,1024,128]{2,1,0:T(8,128)(2,1)S(1)}, u32[]{:S(2)}, u32[]{:S(2)}) %collective-permute-start.32) | collective-permute-done | bytes 524320 | tf_op jit(solution)/shard_map/ppermute | solution.py:28
  147.2 3.3 %collective-permute-start.33 = (bf16[2,1024,128]{2,1,0:T(8,128)(2,1)S(1)}, bf16[2,1024,128]{2,1,0:T(8,128)(2,1)S(1)}, u32[]{:S(2)}, u32[]{:S(2)}) collective-permute-start(bf16[2,1024,128]{2,1,0:T(8,128)(2,1)S(1)} %pad_maximum_fusion.5), channel_id=1, source_target_pairs={{24,0},{25,1},{26,2},{27,3},{28,4},{29,5},{30,6},{31,7},{0,8},{1,9... | collective-permute-start | bytes 1572872 | tf_op jit(solution)/shard_map/ppermute | solution.py:28
  150.7 5.5 %partial_product.6 = (s16[272,1024]{1,0:T(8,128)(2,1)S(1)}, f32[256,1024]{1,0:T(8,128)S(1)}) custom-call(bf16[512,2048]{1,0:T(8,128)(2,1)S(1)} %pad_maximum_fusion.lhs_ref, bf16[5,1024,128]{2,1,0:T(8,128)(2,1)} %collective-permute-done.9.refs_0_.refs_1_, bf16[1024,128]{1,0:T(8,128)(2,1)S(1)} %collective-permute-done.6.refs_1_, ...), custom_call_target="tpu_custom_call" | custom-call | flops 2147483648 | bytes 6291456 | tf_op jit(solution)/shard_map/partial_product/pallas_call | solution.py:155
  156.3 5.5 %partial_product.7 = (s16[272,1024]{1,0:T(8,128)(2,1)S(1)}, f32[256,1024]{1,0:T(8,128)S(1)}) custom-call(bf16[512,2048]{1,0:T(8,128)(2,1)S(1)} %pad_maximum_fusion.lhs_ref, bf16[5,1024,128]{2,1,0:T(8,128)(2,1)S(1)} %collective-permute-done.16.refs_0_.refs_1_, bf16[5,1024,128]{2,1,0:T(8,128)(2,1)} %collective-permute-done.9.refs_0_.refs_1_, ...), custom_call_target="tpu_custom_call" | custom-call | flops 2147483648 | bytes 6291456 | tf_op jit(solution)/shard_map/partial_product/pallas_call | solution.py:155
  161.8 1.9 collective-permute-start.15
  163.7 0.9 collective-permute-start.21
  164.6 3.8 %partial_product.9 = (s16[272,1024]{1,0:T(8,128)(2,1)S(1)}, f32[256,1024]{1,0:T(8,128)S(1)}) custom-call(bf16[512,2048]{1,0:T(8,128)(2,1)S(1)} %pad_maximum_fusion.lhs_ref, bf16[4,1024,128]{2,1,0:T(8,128)(2,1)S(1)} %collective-permute-done.30.refs_0_, bf16[5,1024,128]{2,1,0:T(8,128)(2,1)S(1)} %collective-permute-done.16.refs_0_.refs_1_, ...), custom_call_target="tpu_custom_call" | custom-call | flops 2147483648 | bytes 6291456 | tf_op jit(solution)/shard_map/partial_product/pallas_call | solution.py:155
  168.4 1.9 collective-permute-start.35
  170.3 7.7 %collective-permute-done.7.refs_2_ = bf16[3,1024,128]{2,1,0:T(8,128)(2,1)S(1)} collective-permute-done((bf16[3,1024,128]{2,1,0:T(8,128)(2,1)S(1)}, bf16[3,1024,128]{2,1,0:T(8,128)(2,1)S(1)}, u32[]{:S(2)}, u32[]{:S(2)}) %collective-permute-start.7) | collective-permute-done | bytes 786464 | tf_op jit(solution)/shard_map/ppermute | solution.py:28
  178.0 1.9 partial_product.5
  179.9 1.9 collective-permute-start.8
  181.8 1.9 partial_product.8
  183.7 0.9 collective-permute-start.27
  184.7 17.0 %collective-permute-done.8.refs_1_ = s16[272,512]{1,0:T(8,128)(2,1)S(1)} collective-permute-done((s16[272,512]{1,0:T(8,128)(2,1)S(1)}, s16[272,512]{1,0:T(8,128)(2,1)S(1)}, u32[]{:S(2)}, u32[]{:S(2)}) %collective-permute-start.8) | collective-permute-done | bytes 278560 | tf_op jit(solution)/shard_map/ppermute | solution.py:28
  202.1 9.4 %collective-permute-start.28 = (bf16[128,1536]{1,0:T(8,128)(2,1)S(1)}, bf16[128,1536]{1,0:T(8,128)(2,1)S(1)}, u32[]{:S(2)}, u32[]{:S(2)}) collective-permute-start(bf16[128,1536]{1,0:T(8,128)(2,1)S(1)} %get-tuple-element.35), channel_id=1, source_target_pairs={{4,0},{5,1},{6,2},{7,3},{0,4},{1,5},{2,6},{3,7},{12,8},{13,9},{14,... | collective-permute-start | bytes 1179656 | tf_op jit(solution)/shard_map/ppermute | solution.py:28
  211.8 2.6 %collective-permute-start.29 = (bf16[128,1536]{1,0:T(8,128)(2,1)S(1)}, bf16[128,1536]{1,0:T(8,128)(2,1)S(1)}, u32[]{:S(2)}, u32[]{:S(2)}) collective-permute-start(bf16[128,1536]{1,0:T(8,128)(2,1)S(1)} %get-tuple-element.36), channel_id=1, source_target_pairs={{4,0},{5,1},{6,2},{7,3},{0,4},{1,5},{2,6},{3,7},{12,8},{13,9},{14,... | collective-permute-start | bytes 1179656 | tf_op jit(solution)/shard_map/ppermute | solution.py:28
  214.8 1.0 collective-permute-done.29.refs_3_
  215.8 2.5 %place.2.refs_0_ = bf16[128,8192]{1,0:T(8,128)(2,1)} custom-call(s32[4,64]{1,0:T(4,128)S(1)} %copy-done.2, bf16[128,1536]{1,0:T(8,128)(2,1)S(1)} %get-tuple-element.29.refs_0_, bf16[128,1536]{1,0:T(8,128)(2,1)S(1)} %get-tuple-element.34.refs_1_, bf16[128,1536]{1,0:T(8,128)(2,1)S(1)} %collective-permute-done.28.refs_2_, ...), custom_call_target="tpu_custom_call" | custom-call | flops 786432 | bytes 3145728 | tf_op jit(solution)/shard_map/place/pallas_call | solution.py:231
  218.3 1.6 place.3
  (82 shorter events, 8.0 us)
Async XLA Ops:
  0.0 0.9 copy-start.1
  1.0 0.7 copy-start.4
  2.2 6.9 %collective-permute-start.5 = (bf16[1024,128]{1,0:T(8,128)(2,1)S(1)}, bf16[1024,128]{1,0:T(8,128)(2,1)S(1)}, u32[]{:S(2)}, u32[]{:S(2)}) collective-permute-start(bf16[1024,128]{1,0:T(8,128)(2,1)S(1)} %mask_right.1), channel_id=1, source_target_pairs={{1,0},{0,1},{3,2},{2,3},{5,4},{4,5},{7,6},{6,7},{9,8},{8,9},{11,10... | collective-permute-start | bytes 786440 | tf_op jit(solution)/shard_map/ppermute | solution.py:28
  4.3 11.6 %collective-permute-start.2 = (bf16[1024,128]{1,0:T(8,128)(2,1)S(1)}, bf16[1024,128]{1,0:T(8,128)(2,1)S(1)}, u32[]{:S(2)}, u32[]{:S(2)}) collective-permute-start(bf16[1024,128]{1,0:T(8,128)(2,1)S(1)} %mask_right.1), channel_id=1, source_target_pairs={{8,0},{9,1},{10,2},{11,3},{12,4},{13,5},{14,6},{15,7},{16,8},{17,9... | collective-permute-start | bytes 786440 | tf_op jit(solution)/shard_map/ppermute | solution.py:28
  7.0 8.9 %collective-permute-start.3 = (bf16[1024,128]{1,0:T(8,128)(2,1)S(1)}, bf16[1024,128]{1,0:T(8,128)(2,1)S(1)}, u32[]{:S(2)}, u32[]{:S(2)}) collective-permute-start(bf16[1024,128]{1,0:T(8,128)(2,1)S(1)} %mask_right.1), channel_id=1, source_target_pairs={{16,0},{17,1},{18,2},{19,3},{20,4},{21,5},{22,6},{23,7},{24,8},{25... | collective-permute-start | bytes 786440 | tf_op jit(solution)/shard_map/ppermute | solution.py:28
  7.4 15.0 %collective-permute-start.4 = (bf16[1024,128]{1,0:T(8,128)(2,1)S(1)}, bf16[1024,128]{1,0:T(8,128)(2,1)S(1)}, u32[]{:S(2)}, u32[]{:S(2)}) collective-permute-start(bf16[1024,128]{1,0:T(8,128)(2,1)S(1)} %mask_right.1), channel_id=1, source_target_pairs={{24,0},{25,1},{26,2},{27,3},{28,4},{29,5},{30,6},{31,7},{0,8},{1,9... | collective-permute-start | bytes 786440 | tf_op jit(solution)/shard_map/ppermute | solution.py:28
  9.1 15.2 %collective-permute-start.6 = (bf16[1024,128]{1,0:T(8,128)(2,1)S(1)}, bf16[1024,128]{1,0:T(8,128)(2,1)S(1)}, u32[]{:S(2)}, u32[]{:S(2)}) collective-permute-start(bf16[1024,128]{1,0:T(8,128)(2,1)S(1)} %collective-permute-done.5.refs_1_), channel_id=1, source_target_pairs={{32,0},{33,1},{34,2},{35,3},{36,4},{37,5},{38,6},{39,7},{40,8},{41... | collective-permute-start | bytes 786440 | tf_op jit(solution)/shard_map/ppermute | solution.py:28
  15.9 14.1 %collective-permute-start.10 = (bf16[1024,128]{1,0:T(8,128)(2,1)S(1)}, bf16[1024,128]{1,0:T(8,128)(2,1)S(1)}, u32[]{:S(2)}, u32[]{:S(2)}) collective-permute-start(bf16[1024,128]{1,0:T(8,128)(2,1)S(1)} %collective-permute-done.5.refs_1_), channel_id=1, source_target_pairs={{224,0},{225,1},{226,2},{227,3},{228,4},{229,5},{230,6},{231,7},{2... | collective-permute-start | bytes 786440 | tf_op jit(solution)/shard_map/ppermute | solution.py:28
  15.9 6.5 %copy-start.5 = (bf16[1024,128]{1,0:T(8,128)(2,1)}, bf16[1024,128]{1,0:T(8,128)(2,1)S(1)}, u32[]{:S(2)}) copy-start(bf16[1024,128]{1,0:T(8,128)(2,1)S(1)} %collective-permute-done.2) | copy-start | bytes 786436
  15.9 6.5 %copy-start.7 = (bf16[1024,128]{1,0:T(8,128)(2,1)}, bf16[1024,128]{1,0:T(8,128)(2,1)S(1)}, u32[]{:S(2)}) copy-start(bf16[1024,128]{1,0:T(8,128)(2,1)S(1)} %collective-permute-done.3) | copy-start | bytes 786436
  22.4 0.7 copy-start.9
  23.2 7.6 %copy-start = (bf16[512,1024]{1,0:T(8,128)(2,1)S(1)}, bf16[512,1024]{1,0:T(8,128)(2,1)}, u32[]{:S(2)}) copy-start(bf16[512,1024]{1,0:T(8,128)(2,1)} %b_ref.1) | copy-start | bytes 3145732
  23.2 7.6 %copy-start.3 = (s32[4,8]{1,0:T(4,128)S(1)}, s32[4,8]{1,0:T(4,128)}, u32[]{:S(2)}) copy-start(s32[4,8]{1,0:T(4,128)} %mask_ref.3) | copy-start | bytes 388
  24.3 44.1 %collective-permute-start.9 = (bf16[5,1024,128]{2,1,0:T(8,128)(2,1)S(1)}, bf16[5,1024,128]{2,1,0:T(8,128)(2,1)}, u32[]{:S(2)}, u32[]{:S(2)}) collective-permute-start(bf16[5,1024,128]{2,1,0:T(8,128)(2,1)S(1)} %constant_dynamic-update-slice_fusion.2.refs_0_), channel_id=1, source_target_pairs={{32,0},{33,1},{34,2},{35,3},{36,4},{37,5},{38,6},{39,7},{40,8},{41... | collective-permute-start | bytes 3932168 | tf_op jit(solution)/shard_map/ppermute | solution.py:28
  30.7 41.5 %collective-permute-start.14 = (bf16[5,1024,128]{2,1,0:T(8,128)(2,1)}, bf16[5,1024,128]{2,1,0:T(8,128)(2,1)}, u32[]{:S(2)}, u32[]{:S(2)}) collective-permute-start(bf16[5,1024,128]{2,1,0:T(8,128)(2,1)} %constant_dynamic-update-slice_fusion.6), channel_id=1, source_target_pairs={{224,0},{225,1},{226,2},{227,3},{228,4},{229,5},{230,6},{231,7},{2... | collective-permute-start | bytes 3932168 | tf_op jit(solution)/shard_map/ppermute | solution.py:28
  31.6 42.9 %collective-permute-start = (bf16[256,1024]{1,0:T(8,128)(2,1)S(1)}, bf16[256,1024]{1,0:T(8,128)(2,1)S(1)}, u32[]{:S(2)}, u32[]{:S(2)}) collective-permute-start(bf16[256,1024]{1,0:T(8,128)(2,1)S(1)} %get-tuple-element.24), channel_id=1, source_target_pairs={{1,0},{0,1},{3,2},{2,3},{5,4},{4,5},{7,6},{6,7},{9,8},{8,9},{11,10... | collective-permute-start | bytes 1572872 | tf_op jit(solution)/shard_map/ppermute | solution.py:28
  32.0 41.0 %collective-permute-start.22 = (bf16[1024,128]{1,0:T(8,128)(2,1)S(1)}, bf16[1024,128]{1,0:T(8,128)(2,1)S(1)}, u32[]{:S(2)}, u32[]{:S(2)}) collective-permute-start(bf16[1024,128]{1,0:T(8,128)(2,1)S(1)} %mask_right.1), channel_id=1, source_target_pairs={{128,0},{129,1},{130,2},{131,3},{132,4},{133,5},{134,6},{135,7},{1... | collective-permute-start | bytes 786440 | tf_op jit(solution)/shard_map/ppermute | solution.py:28
  68.3 40.1 %collective-permute-start.16 = (bf16[5,1024,128]{2,1,0:T(8,128)(2,1)}, bf16[5,1024,128]{2,1,0:T(8,128)(2,1)S(1)}, u32[]{:S(2)}, u32[]{:S(2)}) collective-permute-start(bf16[5,1024,128]{2,1,0:T(8,128)(2,1)} %collective-permute-done.9.refs_0_.refs_1_), channel_id=1, source_target_pairs={{32,0},{33,1},{34,2},{35,3},{36,4},{37,5},{38,6},{39,7},{40,8},{41... | collective-permute-start | bytes 3932168 | tf_op jit(solution)/shard_map/ppermute | solution.py:28
  72.1 36.4 %collective-permute-start.20 = (bf16[5,1024,128]{2,1,0:T(8,128)(2,1)}, bf16[5,1024,128]{2,1,0:T(8,128)(2,1)S(1)}, u32[]{:S(2)}, u32[]{:S(2)}) collective-permute-start(bf16[5,1024,128]{2,1,0:T(8,128)(2,1)} %collective-permute-done.14.refs_5_.refs_6_), channel_id=1, source_target_pairs={{224,0},{225,1},{226,2},{227,3},{228,4},{229,5},{230,6},{231,7},{2... | collective-permute-start | bytes 3932168 | tf_op jit(solution)/shard_map/ppermute | solution.py:28
  73.0 5.5 %collective-permute-start.23 = (bf16[1024,128]{1,0:T(8,128)(2,1)S(1)}, bf16[1024,128]{1,0:T(8,128)(2,1)S(1)}, u32[]{:S(2)}, u32[]{:S(2)}) collective-permute-start(bf16[1024,128]{1,0:T(8,128)(2,1)S(1)} %collective-permute-done.22.refs_0_), channel_id=1, source_target_pairs={{8,0},{9,1},{10,2},{11,3},{12,4},{13,5},{14,6},{15,7},{16,8},{17,9... | collective-permute-start | bytes 786440 | tf_op jit(solution)/shard_map/ppermute | solution.py:28
  73.0 8.7 %collective-permute-start.25 = (bf16[1024,128]{1,0:T(8,128)(2,1)S(1)}, bf16[1024,128]{1,0:T(8,128)(2,1)S(1)}, u32[]{:S(2)}, u32[]{:S(2)}) collective-permute-start(bf16[1024,128]{1,0:T(8,128)(2,1)S(1)} %collective-permute-done.22.refs_0_), channel_id=1, source_target_pairs={{24,0},{25,1},{26,2},{27,3},{28,4},{29,5},{30,6},{31,7},{0,8},{1,9... | collective-permute-start | bytes 786440 | tf_op jit(solution)/shard_map/ppermute | solution.py:28
  74.6 15.1 %collective-permute-start.24 = (bf16[1024,128]{1,0:T(8,128)(2,1)S(1)}, bf16[1024,128]{1,0:T(8,128)(2,1)S(1)}, u32[]{:S(2)}, u32[]{:S(2)}) collective-permute-start(bf16[1024,128]{1,0:T(8,128)(2,1)S(1)} %collective-permute-done.22.refs_0_), channel_id=1, source_target_pairs={{16,0},{17,1},{18,2},{19,3},{20,4},{21,5},{22,6},{23,7},{24,8},{25... | collective-permute-start | bytes 786440 | tf_op jit(solution)/shard_map/ppermute | solution.py:28
  78.5 16.3 %collective-permute-start.11 = (bf16[2,1024,128]{2,1,0:T(8,128)(2,1)S(1)}, bf16[2,1024,128]{2,1,0:T(8,128)(2,1)S(1)}, u32[]{:S(2)}, u32[]{:S(2)}) collective-permute-start(bf16[2,1024,128]{2,1,0:T(8,128)(2,1)S(1)} %pad_maximum_fusion.3), channel_id=1, source_target_pairs={{8,0},{9,1},{10,2},{11,3},{12,4},{13,5},{14,6},{15,7},{16,8},{17,9... | collective-permute-start | bytes 1572872 | tf_op jit(solution)/shard_map/ppermute | solution.py:28
  81.7 33.9 %collective-permute-start.1 = (bf16[256,2048]{1,0:T(8,128)(2,1)S(1)}, bf16[256,2048]{1,0:T(8,128)(2,1)S(1)}, u32[]{:S(2)}, u32[]{:S(2)}) collective-permute-start(bf16[256,2048]{1,0:T(8,128)(2,1)S(1)} %constant_dynamic-update-slice_fusion), channel_id=1, source_target_pairs={{4,0},{5,1},{6,2},{7,3},{0,4},{1,5},{2,6},{3,7},{12,8},{13,9},{14,... | collective-permute-start | bytes 3145736 | tf_op jit(solution)/shard_map/ppermute | solution.py:28
  89.6 14.9 %collective-permute-start.12 = (bf16[2,1024,128]{2,1,0:T(8,128)(2,1)S(1)}, bf16[2,1024,128]{2,1,0:T(8,128)(2,1)S(1)}, u32[]{:S(2)}, u32[]{:S(2)}) collective-permute-start(bf16[2,1024,128]{2,1,0:T(8,128)(2,1)S(1)} %pad_maximum_fusion.3), channel_id=1, source_target_pairs={{16,0},{17,1},{18,2},{19,3},{20,4},{21,5},{22,6},{23,7},{24,8},{25... | collective-permute-start | bytes 1572872 | tf_op jit(solution)/shard_map/ppermute | solution.py:28
  94.9 20.7 %collective-permute-start.13 = (bf16[2,1024,128]{2,1,0:T(8,128)(2,1)S(1)}, bf16[2,1024,128]{2,1,0:T(8,128)(2,1)S(1)}, u32[]{:S(2)}, u32[]{:S(2)}) collective-permute-start(bf16[2,1024,128]{2,1,0:T(8,128)(2,1)S(1)} %pad_maximum_fusion.3), channel_id=1, source_target_pairs={{24,0},{25,1},{26,2},{27,3},{28,4},{29,5},{30,6},{31,7},{0,8},{1,9... | collective-permute-start | bytes 1572872 | tf_op jit(solution)/shard_map/ppermute | solution.py:28
  104.6 12.9 %collective-permute-start.17 = (bf16[2,1024,128]{2,1,0:T(8,128)(2,1)S(1)}, bf16[2,1024,128]{2,1,0:T(8,128)(2,1)S(1)}, u32[]{:S(2)}, u32[]{:S(2)}) collective-permute-start(bf16[2,1024,128]{2,1,0:T(8,128)(2,1)S(1)} %pad_maximum_fusion.4), channel_id=1, source_target_pairs={{8,0},{9,1},{10,2},{11,3},{12,4},{13,5},{14,6},{15,7},{16,8},{17,9... | collective-permute-start | bytes 1572872 | tf_op jit(solution)/shard_map/ppermute | solution.py:28
  108.5 16.3 %collective-permute-start.18 = (bf16[2,1024,128]{2,1,0:T(8,128)(2,1)S(1)}, bf16[2,1024,128]{2,1,0:T(8,128)(2,1)S(1)}, u32[]{:S(2)}, u32[]{:S(2)}) collective-permute-start(bf16[2,1024,128]{2,1,0:T(8,128)(2,1)S(1)} %pad_maximum_fusion.4), channel_id=1, source_target_pairs={{16,0},{17,1},{18,2},{19,3},{20,4},{21,5},{22,6},{23,7},{24,8},{25... | collective-permute-start | bytes 1572872 | tf_op jit(solution)/shard_map/ppermute | solution.py:28
  108.5 30.7 %collective-permute-start.19 = (bf16[2,1024,128]{2,1,0:T(8,128)(2,1)S(1)}, bf16[2,1024,128]{2,1,0:T(8,128)(2,1)S(1)}, u32[]{:S(2)}, u32[]{:S(2)}) collective-permute-start(bf16[2,1024,128]{2,1,0:T(8,128)(2,1)S(1)} %pad_maximum_fusion.4), channel_id=1, source_target_pairs={{24,0},{25,1},{26,2},{27,3},{28,4},{29,5},{30,6},{31,7},{0,8},{1,9... | collective-permute-start | bytes 1572872 | tf_op jit(solution)/shard_map/ppermute | solution.py:28
  115.6 24.4 %collective-permute-start.31 = (bf16[2,1024,128]{2,1,0:T(8,128)(2,1)S(1)}, bf16[2,1024,128]{2,1,0:T(8,128)(2,1)S(1)}, u32[]{:S(2)}, u32[]{:S(2)}) collective-permute-start(bf16[2,1024,128]{2,1,0:T(8,128)(2,1)S(1)} %pad_maximum_fusion.5), channel_id=1, source_target_pairs={{8,0},{9,1},{10,2},{11,3},{12,4},{13,5},{14,6},{15,7},{16,8},{17,9... | collective-permute-start | bytes 1572872 | tf_op jit(solution)/shard_map/ppermute | solution.py:28
  115.6 31.6 %collective-permute-start.32 = (bf16[2,1024,128]{2,1,0:T(8,128)(2,1)S(1)}, bf16[2,1024,128]{2,1,0:T(8,128)(2,1)S(1)}, u32[]{:S(2)}, u32[]{:S(2)}) collective-permute-start(bf16[2,1024,128]{2,1,0:T(8,128)(2,1)S(1)} %pad_maximum_fusion.5), channel_id=1, source_target_pairs={{16,0},{17,1},{18,2},{19,3},{20,4},{21,5},{22,6},{23,7},{24,8},{25... | collective-permute-start | bytes 1572872 | tf_op jit(solution)/shard_map/ppermute | solution.py:28
  117.4 46.3 %collective-permute-start.30 = (bf16[4,1024,128]{2,1,0:T(8,128)(2,1)S(1)}, bf16[4,1024,128]{2,1,0:T(8,128)(2,1)S(1)}, u32[]{:S(2)}, u32[]{:S(2)}) collective-permute-start(bf16[4,1024,128]{2,1,0:T(8,128)(2,1)S(1)} %slice.26), channel_id=1, source_target_pairs={{32,0},{33,1},{34,2},{35,3},{36,4},{37,5},{38,6},{39,7},{40,8},{41... | collective-permute-start | bytes 3145736 | tf_op jit(solution)/shard_map/ppermute | solution.py:28
  120.3 19.2 %copy-start.6 = (bf16[1024,128]{1,0:T(8,128)(2,1)S(1)}, bf16[1024,128]{1,0:T(8,128)(2,1)}, u32[]{:S(2)}) copy-start(bf16[1024,128]{1,0:T(8,128)(2,1)} %copy-done.5) | copy-start | bytes 786436
  120.3 19.2 %copy-start.8 = (bf16[1024,128]{1,0:T(8,128)(2,1)S(1)}, bf16[1024,128]{1,0:T(8,128)(2,1)}, u32[]{:S(2)}) copy-start(bf16[1024,128]{1,0:T(8,128)(2,1)} %copy-done.7) | copy-start | bytes 786436
  120.3 19.2 %copy-start.10 = (bf16[1024,128]{1,0:T(8,128)(2,1)S(1)}, bf16[1024,128]{1,0:T(8,128)(2,1)}, u32[]{:S(2)}) copy-start(bf16[1024,128]{1,0:T(8,128)(2,1)} %copy-done.9) | copy-start | bytes 786436
  124.7 39.8 %collective-permute-start.34 = (bf16[4,1024,128]{2,1,0:T(8,128)(2,1)S(1)}, bf16[4,1024,128]{2,1,0:T(8,128)(2,1)S(1)}, u32[]{:S(2)}, u32[]{:S(2)}) collective-permute-start(bf16[4,1024,128]{2,1,0:T(8,128)(2,1)S(1)} %slice.29), channel_id=1, source_target_pairs={{224,0},{225,1},{226,2},{227,3},{228,4},{229,5},{230,6},{231,7},{2... | collective-permute-start | bytes 3145736 | tf_op jit(solution)/shard_map/ppermute | solution.py:28
  139.2 42.6 %collective-permute-start.26 = (bf16[4,1024,128]{2,1,0:T(8,128)(2,1)S(1)}, bf16[4,1024,128]{2,1,0:T(8,128)(2,1)S(1)}, u32[]{:S(2)}, u32[]{:S(2)}) collective-permute-start(bf16[4,1024,128]{2,1,0:T(8,128)(2,1)S(1)} %pad_maximum_fusion.1), channel_id=1, source_target_pairs={{1,0},{0,1},{3,2},{2,3},{5,4},{4,5},{7,6},{6,7},{9,8},{8,9},{11,10... | collective-permute-start | bytes 3145736 | tf_op jit(solution)/shard_map/ppermute | solution.py:28
  139.9 38.1 %collective-permute-start.7 = (bf16[3,1024,128]{2,1,0:T(8,128)(2,1)S(1)}, bf16[3,1024,128]{2,1,0:T(8,128)(2,1)S(1)}, u32[]{:S(2)}, u32[]{:S(2)}) collective-permute-start(bf16[3,1024,128]{2,1,0:T(8,128)(2,1)S(1)} %pad_maximum_fusion.2), channel_id=1, source_target_pairs={{1,0},{0,1},{3,2},{2,3},{5,4},{4,5},{7,6},{6,7},{9,8},{8,9},{11,10... | collective-permute-start | bytes 2359304 | tf_op jit(solution)/shard_map/ppermute | solution.py:28
  147.2 14.6 %collective-permute-start.33 = (bf16[2,1024,128]{2,1,0:T(8,128)(2,1)S(1)}, bf16[2,1024,128]{2,1,0:T(8,128)(2,1)S(1)}, u32[]{:S(2)}, u32[]{:S(2)}) collective-permute-start(bf16[2,1024,128]{2,1,0:T(8,128)(2,1)S(1)} %pad_maximum_fusion.5), channel_id=1, source_target_pairs={{24,0},{25,1},{26,2},{27,3},{28,4},{29,5},{30,6},{31,7},{0,8},{1,9... | collective-permute-start | bytes 1572872 | tf_op jit(solution)/shard_map/ppermute | solution.py:28
  161.8 39.9 %collective-permute-start.15 = (s16[272,1024]{1,0:T(8,128)(2,1)S(1)}, s16[272,1024]{1,0:T(8,128)(2,1)S(1)}, u32[]{:S(2)}, u32[]{:S(2)}) collective-permute-start(s16[272,1024]{1,0:T(8,128)(2,1)S(1)} %get-tuple-element.28), channel_id=1, source_target_pairs={{3,0},{2,1},{1,2},{0,3},{7,4},{6,5},{5,6},{4,7},{11,8},{10,9},{9,1... | collective-permute-start | bytes 1671176 | tf_op jit(solution)/shard_map/ppermute | solution.py:28
  163.7 47.7 %collective-permute-start.21 = (s16[272,1024]{1,0:T(8,128)(2,1)S(1)}, s16[272,1024]{1,0:T(8,128)(2,1)S(1)}, u32[]{:S(2)}, u32[]{:S(2)}) collective-permute-start(s16[272,1024]{1,0:T(8,128)(2,1)S(1)} %get-tuple-element.31), channel_id=1, source_target_pairs={{3,0},{2,1},{1,2},{0,3},{7,4},{6,5},{5,6},{4,7},{11,8},{10,9},{9,1... | collective-permute-start | bytes 1671176 | tf_op jit(solution)/shard_map/ppermute | solution.py:28
  168.4 46.0 %collective-permute-start.35 = (s16[272,1024]{1,0:T(8,128)(2,1)S(1)}, s16[272,1024]{1,0:T(8,128)(2,1)S(1)}, u32[]{:S(2)}, u32[]{:S(2)}) collective-permute-start(s16[272,1024]{1,0:T(8,128)(2,1)S(1)} %get-tuple-element.38), channel_id=1, source_target_pairs={{3,0},{2,1},{1,2},{0,3},{7,4},{6,5},{5,6},{4,7},{11,8},{10,9},{9,1... | collective-permute-start | bytes 1671176 | tf_op jit(solution)/shard_map/ppermute | solution.py:28
  179.9 21.8 %collective-permute-start.8 = (s16[272,512]{1,0:T(8,128)(2,1)S(1)}, s16[272,512]{1,0:T(8,128)(2,1)S(1)}, u32[]{:S(2)}, u32[]{:S(2)}) collective-permute-start(s16[272,512]{1,0:T(8,128)(2,1)S(1)} %get-tuple-element.26), channel_id=1, source_target_pairs={{3,0},{2,1},{1,2},{0,3},{7,4},{6,5},{5,6},{4,7},{11,8},{10,9},{9,1... | collective-permute-start | bytes 835592 | tf_op jit(solution)/shard_map/ppermute | solution.py:28
  183.7 27.7 %collective-permute-start.27 = (s16[272,512]{1,0:T(8,128)(2,1)S(1)}, s16[272,512]{1,0:T(8,128)(2,1)S(1)}, u32[]{:S(2)}, u32[]{:S(2)}) collective-permute-start(s16[272,512]{1,0:T(8,128)(2,1)S(1)} %get-tuple-element.33), channel_id=1, source_target_pairs={{3,0},{2,1},{1,2},{0,3},{7,4},{6,5},{5,6},{4,7},{11,8},{10,9},{9,1... | collective-permute-start | bytes 835592 | tf_op jit(solution)/shard_map/ppermute | solution.py:28
  202.1 12.7 %collective-permute-start.28 = (bf16[128,1536]{1,0:T(8,128)(2,1)S(1)}, bf16[128,1536]{1,0:T(8,128)(2,1)S(1)}, u32[]{:S(2)}, u32[]{:S(2)}) collective-permute-start(bf16[128,1536]{1,0:T(8,128)(2,1)S(1)} %get-tuple-element.35), channel_id=1, source_target_pairs={{4,0},{5,1},{6,2},{7,3},{0,4},{1,5},{2,6},{3,7},{12,8},{13,9},{14,... | collective-permute-start | bytes 1179656 | tf_op jit(solution)/shard_map/ppermute | solution.py:28
  211.8 4.0 %copy-start.2 = (s32[4,64]{1,0:T(4,128)S(1)}, s32[4,64]{1,0:T(4,128)}, u32[]{:S(2)}) copy-start(s32[4,64]{1,0:T(4,128)} %mask_ref.5) | copy-start | bytes 3076
  211.8 4.0 %collective-permute-start.29 = (bf16[128,1536]{1,0:T(8,128)(2,1)S(1)}, bf16[128,1536]{1,0:T(8,128)(2,1)S(1)}, u32[]{:S(2)}, u32[]{:S(2)}) collective-permute-start(bf16[128,1536]{1,0:T(8,128)(2,1)S(1)} %get-tuple-element.36), channel_id=1, source_target_pairs={{4,0},{5,1},{6,2},{7,3},{0,4},{1,5},{2,6},{3,7},{12,8},{13,9},{14,... | collective-permute-start | bytes 1179656 | tf_op jit(solution)/shard_map/ppermute | solution.py:28
  214.6 3.6 %collective-permute-start.36 = (bf16[128,1024]{1,0:T(8,128)(2,1)S(1)}, bf16[128,1024]{1,0:T(8,128)(2,1)S(1)}, u32[]{:S(2)}, u32[]{:S(2)}) collective-permute-start(bf16[128,1024]{1,0:T(8,128)(2,1)S(1)} %get-tuple-element.40), channel_id=1, source_target_pairs={{4,0},{5,1},{6,2},{7,3},{0,4},{1,5},{2,6},{3,7},{12,8},{13,9},{14,... | collective-permute-start | bytes 786440 | tf_op jit(solution)/shard_map/ppermute | solution.py:28

commit v2 on v1

--- a/solution.py
+++ b/solution.py
@@ -265,44 +265,33 @@
     mine = mask_right(right_blocks, right_mask.T)
     theirs = from_share(mine)
     along = spread(mine)
-    far = from_z(mine, 4)
     near_along = from_share(jnp.stack(along))
     own = {}
     line = {(0, 0): (theirs, None)}
     for k in range(1, Y):
         line[0, k] = (near_along, k - 1)
 
-    hop = {}
-    for s in (1, -1):
-        first = from_z(theirs, s)
-        line[s, 0] = (first, None)
-        hop[s, 0] = jnp.stack([mine, *along, first])
-        for d in (1, 2):
-            packet = from_z(hop[s, d - 1], s)
-            hop[s, d] = packet
-            for k in range(Y):
-                own[s * d, k] = (packet, k)
-            line[s * (d + 1), 0] = (packet, Y)
-        last = hop[s, 2][:Y]
-        packet = from_z(last, s)
+    hop = {0: jnp.stack([mine, *along])}
+    single = {0: theirs}
+    for d in (1, 2, 3):
+        for s in (1, -1):
+            single[s * d] = from_z(single[s * (d - 1)], s)
+            hop[s * d] = from_z(hop[s * (d - 1)], s)
+    for d, packet in hop.items():
         for k in range(Y):
-            own[s * 3, k] = (packet, k)
-    for k in range(Y):
-        own[0, k] = (hop[1, 0], k)
-
-    def block(pair):
-        array, index = pair
-        return array if index is None else array[index]
+            own[d, k] = (packet, k)
 
     for d in (1, 2, 3):
-        both = jnp.stack([block(line[d, 0]), block(line[-d, 0])])
+        line[d, 0], line[-d, 0] = (single[d], None), (single[-d], None)
+        both = jnp.stack([single[d], single[-d]])
         for k, got in enumerate(spread(both), 1):
             line[d, k], line[-d, k] = (got, 0), (got, 1)
 
+    far = from_z(single[3], 1)
     far_all = [far] + spread(far)
     near_far = from_share(jnp.stack(far_all))
     for k in range(Y):
-        own[4, k], line[4, k] = (far_all[k], None), (near_far, k)
+        line[4, k], own[4, k] = (far_all[k], None), (near_far, k)
 
     own_rows, their_rows = mask_left(left_blocks, left_mask, order)
     half = jnp.concatenate([own_rows, from_share(their_rows)], axis=1)

time: 221 us -> 193 us (0.87)
  waiting for transfers between devices: 120 us -> 70.5 us
  starting transfers between devices: 67.7 us -> 95.3 us
  Pallas kernels: 25.1 us -> 21.7 us
  local copies, waits for them, and re-layouts: 6.47 us -> 3.59 us
    ppermute x37 -> x41, waiting for transfers between devices: 120 us -> 70.5 us  [move(): return lax.ppermute(v, BOTH, pairs)]
    ppermute x37 -> x41, starting transfers between devices: 67.7 us -> 95.3 us  [move(): return lax.ppermute(v, BOTH, pairs)]
    pallas_call x5, Pallas kernels: 18.6 us -> 15.2 us  [partial_product(): pl.pallas_call(body, out_shape=(sent, kept), in_specs=[vmem] * (1 + len(a...]
  transfers between devices with their start and end apart: 37 -> 41, of which waited for: 17 -> 16; matrix products, arithmetic and copies ran while one was open for 2% -> 0% of each run, Pallas kernels for 10% -> 10%
where the time goes in v2:
time: 193 us; the launch traced here: 192 us
  starting transfers between devices  95.3 us (49%)
  waiting for transfers between devices  70.5 us (37%)
  Pallas kernels  21.7 us (11%)
  local copies, waits for them, and re-layouts  3.59 us (2%)
    ppermute x41, starting transfers between devices, move(): return lax.ppermute(v, BOTH, pairs)  95.3 us
    ppermute x41, waiting for transfers between devices, move(): return lax.ppermute(v, BOTH, pairs)  70.5 us
    pallas_call x5, Pallas kernels, partial_product(): pl.pallas_call(body, out_shape=(sent, kept), in_specs=[vmem] * (1 + len(a...  15.2 us
    pallas_call x2, Pallas kernels, place(): pl.pallas_call(body, out_shape=jax.ShapeDtypeStruct((rows, Z * Y * C * BS...  4.07 us
  transfers between devices with their start and end apart: 41, of which 16 were waited for; matrix products, arithmetic and copies ran while one was open for 0% of the time, Pallas kernels for 10%

profile of v2, /device:TPU:1, one launch (start us, length us, event | category | flops | bytes accessed | tf_op | source)
XLA Modules:
  0.0 192.3 jit_solution(12549165876450948967)
XLA Ops:
  2.2 2.1 %collective-permute-start.5 = (bf16[1024,128]{1,0:T(8,128)(2,1)S(1)}, bf16[1024,128]{1,0:T(8,128)(2,1)S(1)}, u32[]{:S(2)}, u32[]{:S(2)}) collective-permute-start(bf16[1024,128]{1,0:T(8,128)(2,1)S(1)} %mask_right.1), channel_id=1, source_target_pairs={{1,0},{0,1},{3,2},{2,3},{5,4},{4,5},{7,6},{6,7},{9,8},{8,9},{11,10... | collective-permute-start | bytes 786440 | tf_op jit(solution)/shard_map/ppermute | solution.py:28
  4.3 4.8 %collective-permute-done.5.refs_1_ = bf16[1024,128]{1,0:T(8,128)(2,1)S(1)} collective-permute-done((bf16[1024,128]{1,0:T(8,128)(2,1)S(1)}, bf16[1024,128]{1,0:T(8,128)(2,1)S(1)}, u32[]{:S(2)}, u32[]{:S(2)}) %collective-permute-start.5) | collective-permute-done | bytes 262176 | tf_op jit(solution)/shard_map/ppermute | solution.py:28
  9.1 6.8 %collective-permute-start.9 = (bf16[1024,128]{1,0:T(8,128)(2,1)S(1)}, bf16[1024,128]{1,0:T(8,128)(2,1)S(1)}, u32[]{:S(2)}, u32[]{:S(2)}) collective-permute-start(bf16[1024,128]{1,0:T(8,128)(2,1)S(1)} %collective-permute-done.5.refs_1_), channel_id=1, source_target_pairs={{32,0},{33,1},{34,2},{35,3},{36,4},{37,5},{38,6},{39,7},{40,8},{41... | collective-permute-start | bytes 786440 | tf_op jit(solution)/shard_map/ppermute | solution.py:28
  16.0 1.2 copy-done
  18.8 1.3 collective-permute-start
  20.1 1.3 collective-permute-start.4
  21.4 2.6 %collective-permute-start.3 = (bf16[1024,128]{1,0:T(8,128)(2,1)S(1)}, bf16[1024,128]{1,0:T(8,128)(2,1)S(1)}, u32[]{:S(2)}, u32[]{:S(2)}) collective-permute-start(bf16[1024,128]{1,0:T(8,128)(2,1)S(1)} %mask_right.1), channel_id=1, source_target_pairs={{16,0},{17,1},{18,2},{19,3},{20,4},{21,5},{22,6},{23,7},{24,8},{25... | collective-permute-start | bytes 786440 | tf_op jit(solution)/shard_map/ppermute | solution.py:28
  24.0 1.1 collective-permute-start.2
  25.1 2.7 %collective-permute-start.17 = (bf16[1024,128]{1,0:T(8,128)(2,1)S(1)}, bf16[1024,128]{1,0:T(8,128)(2,1)S(1)}, u32[]{:S(2)}, u32[]{:S(2)}) collective-permute-start(bf16[1024,128]{1,0:T(8,128)(2,1)S(1)} %collective-permute-done.9.refs_1_), channel_id=1, source_target_pairs={{32,0},{33,1},{34,2},{35,3},{36,4},{37,5},{38,6},{39,7},{40,8},{41... | collective-permute-start | bytes 786440 | tf_op jit(solution)/shard_map/ppermute | solution.py:28
  28.6 5.3 %collective-permute-done.3 = bf16[1024,128]{1,0:T(8,128)(2,1)S(1)} collective-permute-done((bf16[1024,128]{1,0:T(8,128)(2,1)S(1)}, bf16[1024,128]{1,0:T(8,128)(2,1)S(1)}, u32[]{:S(2)}, u32[]{:S(2)}) %collective-permute-start.3) | collective-permute-done | bytes 262176 | tf_op jit(solution)/shard_map/ppermute | solution.py:28
  34.0 2.7 %collective-permute-start.8 = (bf16[4,1024,128]{2,1,0:T(8,128)(2,1)S(1)}, bf16[4,1024,128]{2,1,0:T(8,128)(2,1)S(1)}, u32[]{:S(2)}, u32[]{:S(2)}) collective-permute-start(bf16[4,1024,128]{2,1,0:T(8,128)(2,1)S(1)} %pad_maximum_fusion.1.refs_0_), channel_id=1, source_target_pairs={{32,0},{33,1},{34,2},{35,3},{36,4},{37,5},{38,6},{39,7},{40,8},{41... | collective-permute-start | bytes 3145736 | tf_op jit(solution)/shard_map/ppermute | solution.py:28
  36.8 2.2 %collective-permute-start.12 = (bf16[2,1024,128]{2,1,0:T(8,128)(2,1)S(1)}, bf16[2,1024,128]{2,1,0:T(8,128)(2,1)S(1)}, u32[]{:S(2)}, u32[]{:S(2)}) collective-permute-start(bf16[2,1024,128]{2,1,0:T(8,128)(2,1)S(1)} %pad_maximum_fusion.4), channel_id=1, source_target_pairs={{16,0},{17,1},{18,2},{19,3},{20,4},{21,5},{22,6},{23,7},{24,8},{25... | collective-permute-start | bytes 1572872 | tf_op jit(solution)/shard_map/ppermute | solution.py:28
  39.0 1.3 collective-permute-done.18.refs_6_
  40.4 5.7 %collective-permute-done.11.refs_2_ = bf16[2,1024,128]{2,1,0:T(8,128)(2,1)S(1)} collective-permute-done((bf16[2,1024,128]{2,1,0:T(8,128)(2,1)S(1)}, bf16[2,1024,128]{2,1,0:T(8,128)(2,1)S(1)}, u32[]{:S(2)}, u32[]{:S(2)}) %collective-permute-start.11) | collective-permute-done | bytes 524320 | tf_op jit(solution)/shard_map/ppermute | solution.py:28
  46.1 2.4 %collective-permute-start.24 = (bf16[1024,128]{1,0:T(8,128)(2,1)S(1)}, bf16[1024,128]{1,0:T(8,128)(2,1)S(1)}, u32[]{:S(2)}, u32[]{:S(2)}) collective-permute-start(bf16[1024,128]{1,0:T(8,128)(2,1)S(1)} %collective-permute-done.17.refs_1_), channel_id=1, source_target_pairs={{32,0},{33,1},{34,2},{35,3},{36,4},{37,5},{38,6},{39,7},{40,8},{41... | collective-permute-start | bytes 786440 | tf_op jit(solution)/shard_map/ppermute | solution.py:28
  48.6 9.4 %collective-permute-start.19 = (bf16[2,1024,128]{2,1,0:T(8,128)(2,1)S(1)}, bf16[2,1024,128]{2,1,0:T(8,128)(2,1)S(1)}, u32[]{:S(2)}, u32[]{:S(2)}) collective-permute-start(bf16[2,1024,128]{2,1,0:T(8,128)(2,1)S(1)} %pad_maximum_fusion.5), channel_id=1, source_target_pairs={{8,0},{9,1},{10,2},{11,3},{12,4},{13,5},{14,6},{15,7},{16,8},{17,9... | collective-permute-start | bytes 1572872 | tf_op jit(solution)/shard_map/ppermute | solution.py:28
  57.9 2.9 %collective-permute-done.13.refs_4_ = bf16[2,1024,128]{2,1,0:T(8,128)(2,1)S(1)} collective-permute-done((bf16[2,1024,128]{2,1,0:T(8,128)(2,1)S(1)}, bf16[2,1024,128]{2,1,0:T(8,128)(2,1)S(1)}, u32[]{:S(2)}, u32[]{:S(2)}) %collective-permute-start.13) | collective-permute-done | bytes 524320 | tf_op jit(solution)/shard_map/ppermute | solution.py:28
  60.9 3.9 %collective-permute-start.20 = (bf16[2,1024,128]{2,1,0:T(8,128)(2,1)S(1)}, bf16[2,1024,128]{2,1,0:T(8,128)(2,1)S(1)}, u32[]{:S(2)}, u32[]{:S(2)}) collective-permute-start(bf16[2,1024,128]{2,1,0:T(8,128)(2,1)S(1)} %pad_maximum_fusion.5), channel_id=1, source_target_pairs={{16,0},{17,1},{18,2},{19,3},{20,4},{21,5},{22,6},{23,7},{24,8},{25... | collective-permute-start | bytes 1572872 | tf_op jit(solution)/shard_map/ppermute | solution.py:28
  64.8 7.5 %collective-permute-done.34.refs_6_ = bf16[1024,128]{1,0:T(8,128)(2,1)S(1)} collective-permute-done((bf16[1024,128]{1,0:T(8,128)(2,1)S(1)}, bf16[1024,128]{1,0:T(8,128)(2,1)S(1)}, u32[]{:S(2)}, u32[]{:S(2)}) %collective-permute-start.34) | collective-permute-done | bytes 262176 | tf_op jit(solution)/shard_map/ppermute | solution.py:28
  72.5 1.8 collective-permute-start.25
  74.3 1.4 collective-permute-start.22
  75.8 5.7 %collective-permute-start.1 = (bf16[256,2048]{1,0:T(8,128)(2,1)S(1)}, bf16[256,2048]{1,0:T(8,128)(2,1)S(1)}, u32[]{:S(2)}, u32[]{:S(2)}) collective-permute-start(bf16[256,2048]{1,0:T(8,128)(2,1)S(1)} %constant_dynamic-update-slice_fusion), channel_id=1, source_target_pairs={{4,0},{5,1},{6,2},{7,3},{0,4},{1,5},{2,6},{3,7},{12,8},{13,9},{14,... | collective-permute-start | bytes 3145736 | tf_op jit(solution)/shard_map/ppermute | solution.py:28
  81.5 2.5 %collective-permute-start.28 = (bf16[1024,128]{1,0:T(8,128)(2,1)S(1)}, bf16[1024,128]{1,0:T(8,128)(2,1)S(1)}, u32[]{:S(2)}, u32[]{:S(2)}) collective-permute-start(bf16[1024,128]{1,0:T(8,128)(2,1)S(1)} %collective-permute-done.25.refs_1_), channel_id=1, source_target_pairs={{24,0},{25,1},{26,2},{27,3},{28,4},{29,5},{30,6},{31,7},{0,8},{1,9... | collective-permute-start | bytes 786440 | tf_op jit(solution)/shard_map/ppermute | solution.py:28
  84.1 3.8 %collective-permute-done.21.refs_4_ = bf16[2,1024,128]{2,1,0:T(8,128)(2,1)S(1)} collective-permute-done((bf16[2,1024,128]{2,1,0:T(8,128)(2,1)S(1)}, bf16[2,1024,128]{2,1,0:T(8,128)(2,1)S(1)}, u32[]{:S(2)}, u32[]{:S(2)}) %collective-permute-start.21) | collective-permute-done | bytes 524320 | tf_op jit(solution)/shard_map/ppermute | solution.py:28
  87.9 3.1 %collective-permute-start.27 = (bf16[1024,128]{1,0:T(8,128)(2,1)S(1)}, bf16[1024,128]{1,0:T(8,128)(2,1)S(1)}, u32[]{:S(2)}, u32[]{:S(2)}) collective-permute-start(bf16[1024,128]{1,0:T(8,128)(2,1)S(1)} %collective-permute-done.25.refs_1_), channel_id=1, source_target_pairs={{16,0},{17,1},{18,2},{19,3},{20,4},{21,5},{22,6},{23,7},{24,8},{25... | collective-permute-start | bytes 786440 | tf_op jit(solution)/shard_map/ppermute | solution.py:28
  90.9 3.1 %collective-permute-done.28.refs_4_ = bf16[1024,128]{1,0:T(8,128)(2,1)S(1)} collective-permute-done((bf16[1024,128]{1,0:T(8,128)(2,1)S(1)}, bf16[1024,128]{1,0:T(8,128)(2,1)S(1)}, u32[]{:S(2)}, u32[]{:S(2)}) %collective-permute-start.28) | collective-permute-done | bytes 262176 | tf_op jit(solution)/shard_map/ppermute | solution.py:28
  94.1 4.0 %collective-permute-done.27.refs_3_ = bf16[1024,128]{1,0:T(8,128)(2,1)S(1)} collective-permute-done((bf16[1024,128]{1,0:T(8,128)(2,1)S(1)}, bf16[1024,128]{1,0:T(8,128)(2,1)S(1)}, u32[]{:S(2)}, u32[]{:S(2)}) %collective-permute-start.27) | collective-permute-done | bytes 262176 | tf_op jit(solution)/shard_map/ppermute | solution.py:28
  98.1 1.4 collective-permute-done.26.refs_2_
  99.6 4.0 %collective-permute-start.36 = (bf16[2,1024,128]{2,1,0:T(8,128)(2,1)S(1)}, bf16[2,1024,128]{2,1,0:T(8,128)(2,1)S(1)}, u32[]{:S(2)}, u32[]{:S(2)}) collective-permute-start(bf16[2,1024,128]{2,1,0:T(8,128)(2,1)S(1)} %pad_maximum_fusion.6), channel_id=1, source_target_pairs={{16,0},{17,1},{18,2},{19,3},{20,4},{21,5},{22,6},{23,7},{24,8},{25... | collective-permute-start | bytes 1572872 | tf_op jit(solution)/shard_map/ppermute | solution.py:28
  103.6 3.6 %collective-permute-start.33 = (bf16[4,1024,128]{2,1,0:T(8,128)(2,1)S(1)}, bf16[4,1024,128]{2,1,0:T(8,128)(2,1)S(1)}, u32[]{:S(2)}, u32[]{:S(2)}) collective-permute-start(bf16[4,1024,128]{2,1,0:T(8,128)(2,1)S(1)} %collective-permute-done.16.refs_0_), channel_id=1, source_target_pairs={{32,0},{33,1},{34,2},{35,3},{36,4},{37,5},{38,6},{39,7},{40,8},{41... | collective-permute-start | bytes 3145736 | tf_op jit(solution)/shard_map/ppermute | solution.py:28
  107.7 1.1 collective-permute-done.35.refs_2_
  109.1 1.1 collective-permute-done.36.refs_3_
  110.1 15.4 %collective-permute-start.37 = (bf16[2,1024,128]{2,1,0:T(8,128)(2,1)S(1)}, bf16[2,1024,128]{2,1,0:T(8,128)(2,1)S(1)}, u32[]{:S(2)}, u32[]{:S(2)}) collective-permute-start(bf16[2,1024,128]{2,1,0:T(8,128)(2,1)S(1)} %pad_maximum_fusion.6), channel_id=1, source_target_pairs={{24,0},{25,1},{26,2},{27,3},{28,4},{29,5},{30,6},{31,7},{0,8},{1,9... | collective-permute-start | bytes 1572872 | tf_op jit(solution)/shard_map/ppermute | solution.py:28
  125.8 3.8 %partial_product.6 = (s16[272,1024]{1,0:T(8,128)(2,1)S(1)}, f32[256,1024]{1,0:T(8,128)S(1)}) custom-call(bf16[512,2048]{1,0:T(8,128)(2,1)S(1)} %pad_maximum_fusion.lhs_ref, bf16[4,1024,128]{2,1,0:T(8,128)(2,1)S(1)} %collective-permute-done.8.refs_0_, bf16[1024,128]{1,0:T(8,128)(2,1)S(1)} %collective-permute-done.9.refs_1_, ...), custom_call_target="tpu_custom_call" | custom-call | flops 2147483648 | bytes 6291456 | tf_op jit(solution)/shard_map/partial_product/pallas_call | solution.py:155
  129.7 3.8 %partial_product.7 = (s16[272,1024]{1,0:T(8,128)(2,1)S(1)}, f32[256,1024]{1,0:T(8,128)S(1)}) custom-call(bf16[512,2048]{1,0:T(8,128)(2,1)S(1)} %pad_maximum_fusion.lhs_ref, bf16[4,1024,128]{2,1,0:T(8,128)(2,1)S(1)} %collective-permute-done.16.refs_0_, bf16[1024,128]{1,0:T(8,128)(2,1)S(1)} %collective-permute-done.17.refs_1_, ...), custom_call_target="tpu_custom_call" | custom-call | flops 2147483648 | bytes 6291456 | tf_op jit(solution)/shard_map/partial_product/pallas_call | solution.py:155
  134.2 1.8 collective-permute-start.15
  136.9 3.8 %partial_product.9 = (s16[272,1024]{1,0:T(8,128)(2,1)S(1)}, f32[256,1024]{1,0:T(8,128)S(1)}) custom-call(bf16[512,2048]{1,0:T(8,128)(2,1)S(1)} %pad_maximum_fusion.lhs_ref, bf16[4,1024,128]{2,1,0:T(8,128)(2,1)S(1)} %collective-permute-done.33.refs_0_, bf16[1024,128]{1,0:T(8,128)(2,1)S(1)} %collective-permute-done.24.refs_1_, ...), custom_call_target="tpu_custom_call" | custom-call | flops 2147483648 | bytes 6291456 | tf_op jit(solution)/shard_map/partial_product/pallas_call | solution.py:155
  140.7 1.9 collective-permute-start.39
  142.6 1.4 collective-permute-done.6.refs_2_
  144.0 1.9 partial_product.5
  145.8 1.9 collective-permute-start.7
  147.7 1.9 partial_product.8
  150.6 25.3 %collective-permute-done.7.refs_1_ = s16[272,512]{1,0:T(8,128)(2,1)S(1)} collective-permute-done((s16[272,512]{1,0:T(8,128)(2,1)S(1)}, s16[272,512]{1,0:T(8,128)(2,1)S(1)}, u32[]{:S(2)}, u32[]{:S(2)}) %collective-permute-start.7) | collective-permute-done | bytes 278560 | tf_op jit(solution)/shard_map/ppermute | solution.py:28
  176.2 7.5 %collective-permute-start.31 = (bf16[128,1536]{1,0:T(8,128)(2,1)S(1)}, bf16[128,1536]{1,0:T(8,128)(2,1)S(1)}, u32[]{:S(2)}, u32[]{:S(2)}) collective-permute-start(bf16[128,1536]{1,0:T(8,128)(2,1)S(1)} %get-tuple-element.35), channel_id=1, source_target_pairs={{4,0},{5,1},{6,2},{7,3},{0,4},{1,5},{2,6},{3,7},{12,8},{13,9},{14,... | collective-permute-start | bytes 1179656 | tf_op jit(solution)/shard_map/ppermute | solution.py:28
  184.1 2.6 %collective-permute-start.32 = (bf16[128,1536]{1,0:T(8,128)(2,1)S(1)}, bf16[128,1536]{1,0:T(8,128)(2,1)S(1)}, u32[]{:S(2)}, u32[]{:S(2)}) collective-permute-start(bf16[128,1536]{1,0:T(8,128)(2,1)S(1)} %get-tuple-element.36), channel_id=1, source_target_pairs={{4,0},{5,1},{6,2},{7,3},{0,4},{1,5},{2,6},{3,7},{12,8},{13,9},{14,... | collective-permute-start | bytes 1179656 | tf_op jit(solution)/shard_map/ppermute | solution.py:28
  187.0 1.0 collective-permute-done.32.refs_3_
  188.0 2.5 %place.2.refs_0_ = bf16[128,8192]{1,0:T(8,128)(2,1)} custom-call(s32[4,64]{1,0:T(4,128)S(1)} %copy-done.2, bf16[128,1536]{1,0:T(8,128)(2,1)S(1)} %get-tuple-element.29.refs_0_, bf16[128,1536]{1,0:T(8,128)(2,1)S(1)} %get-tuple-element.34.refs_1_, bf16[128,1536]{1,0:T(8,128)(2,1)S(1)} %collective-permute-done.31.refs_2_, ...), custom_call_target="tpu_custom_call" | custom-call | flops 786432 | bytes 3145728 | tf_op jit(solution)/shard_map/place/pallas_call | solution.py:231
  190.5 1.6 place.3
  (66 shorter events, 9.9 us)
Async XLA Ops:
  0.0 0.9 copy-start.1
  1.0 0.7 copy-start.4
  2.2 6.9 %collective-permute-start.5 = (bf16[1024,128]{1,0:T(8,128)(2,1)S(1)}, bf16[1024,128]{1,0:T(8,128)(2,1)S(1)}, u32[]{:S(2)}, u32[]{:S(2)}) collective-permute-start(bf16[1024,128]{1,0:T(8,128)(2,1)S(1)} %mask_right.1), channel_id=1, source_target_pairs={{1,0},{0,1},{3,2},{2,3},{5,4},{4,5},{7,6},{6,7},{9,8},{8,9},{11,10... | collective-permute-start | bytes 786440 | tf_op jit(solution)/shard_map/ppermute | solution.py:28
  9.1 14.9 %collective-permute-start.9 = (bf16[1024,128]{1,0:T(8,128)(2,1)S(1)}, bf16[1024,128]{1,0:T(8,128)(2,1)S(1)}, u32[]{:S(2)}, u32[]{:S(2)}) collective-permute-start(bf16[1024,128]{1,0:T(8,128)(2,1)S(1)} %collective-permute-done.5.refs_1_), channel_id=1, source_target_pairs={{32,0},{33,1},{34,2},{35,3},{36,4},{37,5},{38,6},{39,7},{40,8},{41... | collective-permute-start | bytes 786440 | tf_op jit(solution)/shard_map/ppermute | solution.py:28
  15.9 9.2 %collective-permute-start.10 = (bf16[1024,128]{1,0:T(8,128)(2,1)S(1)}, bf16[1024,128]{1,0:T(8,128)(2,1)S(1)}, u32[]{:S(2)}, u32[]{:S(2)}) collective-permute-start(bf16[1024,128]{1,0:T(8,128)(2,1)S(1)} %collective-permute-done.5.refs_1_), channel_id=1, source_target_pairs={{224,0},{225,1},{226,2},{227,3},{228,4},{229,5},{230,6},{231,7},{2... | collective-permute-start | bytes 786440 | tf_op jit(solution)/shard_map/ppermute | solution.py:28
  15.9 1.2 copy-start
  17.2 0.7 copy-start.3
  18.8 18.0 %collective-permute-start = (bf16[256,1024]{1,0:T(8,128)(2,1)S(1)}, bf16[256,1024]{1,0:T(8,128)(2,1)S(1)}, u32[]{:S(2)}, u32[]{:S(2)}) collective-permute-start(bf16[256,1024]{1,0:T(8,128)(2,1)S(1)} %get-tuple-element.24), channel_id=1, source_target_pairs={{1,0},{0,1},{3,2},{2,3},{5,4},{4,5},{7,6},{6,7},{9,8},{8,9},{11,10... | collective-permute-start | bytes 1572872 | tf_op jit(solution)/shard_map/ppermute | solution.py:28
  20.1 7.7 %collective-permute-start.4 = (bf16[1024,128]{1,0:T(8,128)(2,1)S(1)}, bf16[1024,128]{1,0:T(8,128)(2,1)S(1)}, u32[]{:S(2)}, u32[]{:S(2)}) collective-permute-start(bf16[1024,128]{1,0:T(8,128)(2,1)S(1)} %mask_right.1), channel_id=1, source_target_pairs={{24,0},{25,1},{26,2},{27,3},{28,4},{29,5},{30,6},{31,7},{0,8},{1,9... | collective-permute-start | bytes 786440 | tf_op jit(solution)/shard_map/ppermute | solution.py:28
  21.4 12.5 %collective-permute-start.3 = (bf16[1024,128]{1,0:T(8,128)(2,1)S(1)}, bf16[1024,128]{1,0:T(8,128)(2,1)S(1)}, u32[]{:S(2)}, u32[]{:S(2)}) collective-permute-start(bf16[1024,128]{1,0:T(8,128)(2,1)S(1)} %mask_right.1), channel_id=1, source_target_pairs={{16,0},{17,1},{18,2},{19,3},{20,4},{21,5},{22,6},{23,7},{24,8},{25... | collective-permute-start | bytes 786440 | tf_op jit(solution)/shard_map/ppermute | solution.py:28
  24.0 9.9 %collective-permute-start.2 = (bf16[1024,128]{1,0:T(8,128)(2,1)S(1)}, bf16[1024,128]{1,0:T(8,128)(2,1)S(1)}, u32[]{:S(2)}, u32[]{:S(2)}) collective-permute-start(bf16[1024,128]{1,0:T(8,128)(2,1)S(1)} %mask_right.1), channel_id=1, source_target_pairs={{8,0},{9,1},{10,2},{11,3},{12,4},{13,5},{14,6},{15,7},{16,8},{17,9... | collective-permute-start | bytes 786440 | tf_op jit(solution)/shard_map/ppermute | solution.py:28
  25.1 11.8 %collective-permute-start.17 = (bf16[1024,128]{1,0:T(8,128)(2,1)S(1)}, bf16[1024,128]{1,0:T(8,128)(2,1)S(1)}, u32[]{:S(2)}, u32[]{:S(2)}) collective-permute-start(bf16[1024,128]{1,0:T(8,128)(2,1)S(1)} %collective-permute-done.9.refs_1_), channel_id=1, source_target_pairs={{32,0},{33,1},{34,2},{35,3},{36,4},{37,5},{38,6},{39,7},{40,8},{41... | collective-permute-start | bytes 786440 | tf_op jit(solution)/shard_map/ppermute | solution.py:28
  27.8 18.3 %collective-permute-start.11 = (bf16[2,1024,128]{2,1,0:T(8,128)(2,1)S(1)}, bf16[2,1024,128]{2,1,0:T(8,128)(2,1)S(1)}, u32[]{:S(2)}, u32[]{:S(2)}) collective-permute-start(bf16[2,1024,128]{2,1,0:T(8,128)(2,1)S(1)} %pad_maximum_fusion.4), channel_id=1, source_target_pairs={{8,0},{9,1},{10,2},{11,3},{12,4},{13,5},{14,6},{15,7},{16,8},{17,9... | collective-permute-start | bytes 1572872 | tf_op jit(solution)/shard_map/ppermute | solution.py:28
  33.9 6.4 %collective-permute-start.18 = (bf16[1024,128]{1,0:T(8,128)(2,1)S(1)}, bf16[1024,128]{1,0:T(8,128)(2,1)S(1)}, u32[]{:S(2)}, u32[]{:S(2)}) collective-permute-start(bf16[1024,128]{1,0:T(8,128)(2,1)S(1)} %collective-permute-done.10.refs_6_), channel_id=1, source_target_pairs={{224,0},{225,1},{226,2},{227,3},{228,4},{229,5},{230,6},{231,7},{2... | collective-permute-start | bytes 786440 | tf_op jit(solution)/shard_map/ppermute | solution.py:28
  34.0 38.4 %collective-permute-start.8 = (bf16[4,1024,128]{2,1,0:T(8,128)(2,1)S(1)}, bf16[4,1024,128]{2,1,0:T(8,128)(2,1)S(1)}, u32[]{:S(2)}, u32[]{:S(2)}) collective-permute-start(bf16[4,1024,128]{2,1,0:T(8,128)(2,1)S(1)} %pad_maximum_fusion.1.refs_0_), channel_id=1, source_target_pairs={{32,0},{33,1},{34,2},{35,3},{36,4},{37,5},{38,6},{39,7},{40,8},{41... | collective-permute-start | bytes 3145736 | tf_op jit(solution)/shard_map/ppermute | solution.py:28
  36.8 37.5 %collective-permute-start.14 = (bf16[4,1024,128]{2,1,0:T(8,128)(2,1)S(1)}, bf16[4,1024,128]{2,1,0:T(8,128)(2,1)S(1)}, u32[]{:S(2)}, u32[]{:S(2)}) collective-permute-start(bf16[4,1024,128]{2,1,0:T(8,128)(2,1)S(1)} %pad_maximum_fusion.1.refs_0_), channel_id=1, source_target_pairs={{224,0},{225,1},{226,2},{227,3},{228,4},{229,5},{230,6},{231,7},{2... | collective-permute-start | bytes 3145736 | tf_op jit(solution)/shard_map/ppermute | solution.py:28
  36.8 11.8 %collective-permute-start.12 = (bf16[2,1024,128]{2,1,0:T(8,128)(2,1)S(1)}, bf16[2,1024,128]{2,1,0:T(8,128)(2,1)S(1)}, u32[]{:S(2)}, u32[]{:S(2)}) collective-permute-start(bf16[2,1024,128]{2,1,0:T(8,128)(2,1)S(1)} %pad_maximum_fusion.4), channel_id=1, source_target_pairs={{16,0},{17,1},{18,2},{19,3},{20,4},{21,5},{22,6},{23,7},{24,8},{25... | collective-permute-start | bytes 1572872 | tf_op jit(solution)/shard_map/ppermute | solution.py:28
  40.3 20.5 %collective-permute-start.13 = (bf16[2,1024,128]{2,1,0:T(8,128)(2,1)S(1)}, bf16[2,1024,128]{2,1,0:T(8,128)(2,1)S(1)}, u32[]{:S(2)}, u32[]{:S(2)}) collective-permute-start(bf16[2,1024,128]{2,1,0:T(8,128)(2,1)S(1)} %pad_maximum_fusion.4), channel_id=1, source_target_pairs={{24,0},{25,1},{26,2},{27,3},{28,4},{29,5},{30,6},{31,7},{0,8},{1,9... | collective-permute-start | bytes 1572872 | tf_op jit(solution)/shard_map/ppermute | solution.py:28
  46.1 18.7 %collective-permute-start.24 = (bf16[1024,128]{1,0:T(8,128)(2,1)S(1)}, bf16[1024,128]{1,0:T(8,128)(2,1)S(1)}, u32[]{:S(2)}, u32[]{:S(2)}) collective-permute-start(bf16[1024,128]{1,0:T(8,128)(2,1)S(1)} %collective-permute-done.17.refs_1_), channel_id=1, source_target_pairs={{32,0},{33,1},{34,2},{35,3},{36,4},{37,5},{38,6},{39,7},{40,8},{41... | collective-permute-start | bytes 786440 | tf_op jit(solution)/shard_map/ppermute | solution.py:28
  48.6 25.8 %collective-permute-start.19 = (bf16[2,1024,128]{2,1,0:T(8,128)(2,1)S(1)}, bf16[2,1024,128]{2,1,0:T(8,128)(2,1)S(1)}, u32[]{:S(2)}, u32[]{:S(2)}) collective-permute-start(bf16[2,1024,128]{2,1,0:T(8,128)(2,1)S(1)} %pad_maximum_fusion.5), channel_id=1, source_target_pairs={{8,0},{9,1},{10,2},{11,3},{12,4},{13,5},{14,6},{15,7},{16,8},{17,9... | collective-permute-start | bytes 1572872 | tf_op jit(solution)/shard_map/ppermute | solution.py:28
  60.9 14.9 %collective-permute-start.20 = (bf16[2,1024,128]{2,1,0:T(8,128)(2,1)S(1)}, bf16[2,1024,128]{2,1,0:T(8,128)(2,1)S(1)}, u32[]{:S(2)}, u32[]{:S(2)}) collective-permute-start(bf16[2,1024,128]{2,1,0:T(8,128)(2,1)S(1)} %pad_maximum_fusion.5), channel_id=1, source_target_pairs={{16,0},{17,1},{18,2},{19,3},{20,4},{21,5},{22,6},{23,7},{24,8},{25... | collective-permute-start | bytes 1572872 | tf_op jit(solution)/shard_map/ppermute | solution.py:28
  64.8 7.5 %collective-permute-start.34 = (bf16[1024,128]{1,0:T(8,128)(2,1)S(1)}, bf16[1024,128]{1,0:T(8,128)(2,1)S(1)}, u32[]{:S(2)}, u32[]{:S(2)}) collective-permute-start(bf16[1024,128]{1,0:T(8,128)(2,1)S(1)} %collective-permute-done.18.refs_6_), channel_id=1, source_target_pairs={{224,0},{225,1},{226,2},{227,3},{228,4},{229,5},{230,6},{231,7},{2... | collective-permute-start | bytes 786440 | tf_op jit(solution)/shard_map/ppermute | solution.py:28
  72.3 15.5 %collective-permute-start.21 = (bf16[2,1024,128]{2,1,0:T(8,128)(2,1)S(1)}, bf16[2,1024,128]{2,1,0:T(8,128)(2,1)S(1)}, u32[]{:S(2)}, u32[]{:S(2)}) collective-permute-start(bf16[2,1024,128]{2,1,0:T(8,128)(2,1)S(1)} %pad_maximum_fusion.5), channel_id=1, source_target_pairs={{24,0},{25,1},{26,2},{27,3},{28,4},{29,5},{30,6},{31,7},{0,8},{1,9... | collective-permute-start | bytes 1572872 | tf_op jit(solution)/shard_map/ppermute | solution.py:28
  72.5 9.0 %collective-permute-start.25 = (bf16[1024,128]{1,0:T(8,128)(2,1)S(1)}, bf16[1024,128]{1,0:T(8,128)(2,1)S(1)}, u32[]{:S(2)}, u32[]{:S(2)}) collective-permute-start(bf16[1024,128]{1,0:T(8,128)(2,1)S(1)} %collective-permute-done.24.refs_1_), channel_id=1, source_target_pairs={{32,0},{33,1},{34,2},{35,3},{36,4},{37,5},{38,6},{39,7},{40,8},{41... | collective-permute-start | bytes 786440 | tf_op jit(solution)/shard_map/ppermute | solution.py:28
  74.3 29.3 %collective-permute-start.16 = (bf16[4,1024,128]{2,1,0:T(8,128)(2,1)S(1)}, bf16[4,1024,128]{2,1,0:T(8,128)(2,1)S(1)}, u32[]{:S(2)}, u32[]{:S(2)}) collective-permute-start(bf16[4,1024,128]{2,1,0:T(8,128)(2,1)S(1)} %collective-permute-done.8.refs_0_), channel_id=1, source_target_pairs={{32,0},{33,1},{34,2},{35,3},{36,4},{37,5},{38,6},{39,7},{40,8},{41... | collective-permute-start | bytes 3145736 | tf_op jit(solution)/shard_map/ppermute | solution.py:28
  74.3 32.8 %collective-permute-start.22 = (bf16[4,1024,128]{2,1,0:T(8,128)(2,1)S(1)}, bf16[4,1024,128]{2,1,0:T(8,128)(2,1)S(1)}, u32[]{:S(2)}, u32[]{:S(2)}) collective-permute-start(bf16[4,1024,128]{2,1,0:T(8,128)(2,1)S(1)} %collective-permute-done.14.refs_5_), channel_id=1, source_target_pairs={{224,0},{225,1},{226,2},{227,3},{228,4},{229,5},{230,6},{231,7},{2... | collective-permute-start | bytes 3145736 | tf_op jit(solution)/shard_map/ppermute | solution.py:28
  75.8 31.5 %collective-permute-start.1 = (bf16[256,2048]{1,0:T(8,128)(2,1)S(1)}, bf16[256,2048]{1,0:T(8,128)(2,1)S(1)}, u32[]{:S(2)}, u32[]{:S(2)}) collective-permute-start(bf16[256,2048]{1,0:T(8,128)(2,1)S(1)} %constant_dynamic-update-slice_fusion), channel_id=1, source_target_pairs={{4,0},{5,1},{6,2},{7,3},{0,4},{1,5},{2,6},{3,7},{12,8},{13,9},{14,... | collective-permute-start | bytes 3145736 | tf_op jit(solution)/shard_map/ppermute | solution.py:28
  81.5 12.5 %collective-permute-start.28 = (bf16[1024,128]{1,0:T(8,128)(2,1)S(1)}, bf16[1024,128]{1,0:T(8,128)(2,1)S(1)}, u32[]{:S(2)}, u32[]{:S(2)}) collective-permute-start(bf16[1024,128]{1,0:T(8,128)(2,1)S(1)} %collective-permute-done.25.refs_1_), channel_id=1, source_target_pairs={{24,0},{25,1},{26,2},{27,3},{28,4},{29,5},{30,6},{31,7},{0,8},{1,9... | collective-permute-start | bytes 786440 | tf_op jit(solution)/shard_map/ppermute | solution.py:28
  87.9 10.3 %collective-permute-start.27 = (bf16[1024,128]{1,0:T(8,128)(2,1)S(1)}, bf16[1024,128]{1,0:T(8,128)(2,1)S(1)}, u32[]{:S(2)}, u32[]{:S(2)}) collective-permute-start(bf16[1024,128]{1,0:T(8,128)(2,1)S(1)} %collective-permute-done.25.refs_1_), channel_id=1, source_target_pairs={{16,0},{17,1},{18,2},{19,3},{20,4},{21,5},{22,6},{23,7},{24,8},{25... | collective-permute-start | bytes 786440 | tf_op jit(solution)/shard_map/ppermute | solution.py:28
  94.0 5.5 %collective-permute-start.26 = (bf16[1024,128]{1,0:T(8,128)(2,1)S(1)}, bf16[1024,128]{1,0:T(8,128)(2,1)S(1)}, u32[]{:S(2)}, u32[]{:S(2)}) collective-permute-start(bf16[1024,128]{1,0:T(8,128)(2,1)S(1)} %collective-permute-done.25.refs_1_), channel_id=1, source_target_pairs={{8,0},{9,1},{10,2},{11,3},{12,4},{13,5},{14,6},{15,7},{16,8},{17,9... | collective-permute-start | bytes 786440 | tf_op jit(solution)/shard_map/ppermute | solution.py:28
  98.1 10.7 %collective-permute-start.35 = (bf16[2,1024,128]{2,1,0:T(8,128)(2,1)S(1)}, bf16[2,1024,128]{2,1,0:T(8,128)(2,1)S(1)}, u32[]{:S(2)}, u32[]{:S(2)}) collective-permute-start(bf16[2,1024,128]{2,1,0:T(8,128)(2,1)S(1)} %pad_maximum_fusion.6), channel_id=1, source_target_pairs={{8,0},{9,1},{10,2},{11,3},{12,4},{13,5},{14,6},{15,7},{16,8},{17,9... | collective-permute-start | bytes 1572872 | tf_op jit(solution)/shard_map/ppermute | solution.py:28
  99.6 10.6 %collective-permute-start.36 = (bf16[2,1024,128]{2,1,0:T(8,128)(2,1)S(1)}, bf16[2,1024,128]{2,1,0:T(8,128)(2,1)S(1)}, u32[]{:S(2)}, u32[]{:S(2)}) collective-permute-start(bf16[2,1024,128]{2,1,0:T(8,128)(2,1)S(1)} %pad_maximum_fusion.6), channel_id=1, source_target_pairs={{16,0},{17,1},{18,2},{19,3},{20,4},{21,5},{22,6},{23,7},{24,8},{25... | collective-permute-start | bytes 1572872 | tf_op jit(solution)/shard_map/ppermute | solution.py:28
  103.6 32.4 %collective-permute-start.33 = (bf16[4,1024,128]{2,1,0:T(8,128)(2,1)S(1)}, bf16[4,1024,128]{2,1,0:T(8,128)(2,1)S(1)}, u32[]{:S(2)}, u32[]{:S(2)}) collective-permute-start(bf16[4,1024,128]{2,1,0:T(8,128)(2,1)S(1)} %collective-permute-done.16.refs_0_), channel_id=1, source_target_pairs={{32,0},{33,1},{34,2},{35,3},{36,4},{37,5},{38,6},{39,7},{40,8},{41... | collective-permute-start | bytes 3145736 | tf_op jit(solution)/shard_map/ppermute | solution.py:28
  107.1 29.7 %collective-permute-start.38 = (bf16[4,1024,128]{2,1,0:T(8,128)(2,1)S(1)}, bf16[4,1024,128]{2,1,0:T(8,128)(2,1)S(1)}, u32[]{:S(2)}, u32[]{:S(2)}) collective-permute-start(bf16[4,1024,128]{2,1,0:T(8,128)(2,1)S(1)} %collective-permute-done.22.refs_5_), channel_id=1, source_target_pairs={{224,0},{225,1},{226,2},{227,3},{228,4},{229,5},{230,6},{231,7},{2... | collective-permute-start | bytes 3145736 | tf_op jit(solution)/shard_map/ppermute | solution.py:28
  107.3 40.5 %collective-permute-start.29 = (bf16[4,1024,128]{2,1,0:T(8,128)(2,1)S(1)}, bf16[4,1024,128]{2,1,0:T(8,128)(2,1)S(1)}, u32[]{:S(2)}, u32[]{:S(2)}) collective-permute-start(bf16[4,1024,128]{2,1,0:T(8,128)(2,1)S(1)} %pad_maximum_fusion.2), channel_id=1, source_target_pairs={{1,0},{0,1},{3,2},{2,3},{5,4},{4,5},{7,6},{6,7},{9,8},{8,9},{11,10... | collective-permute-start | bytes 3145736 | tf_op jit(solution)/shard_map/ppermute | solution.py:28
  108.8 35.1 %collective-permute-start.6 = (bf16[3,1024,128]{2,1,0:T(8,128)(2,1)S(1)}, bf16[3,1024,128]{2,1,0:T(8,128)(2,1)S(1)}, u32[]{:S(2)}, u32[]{:S(2)}) collective-permute-start(bf16[3,1024,128]{2,1,0:T(8,128)(2,1)S(1)} %pad_maximum_fusion.3), channel_id=1, source_target_pairs={{1,0},{0,1},{3,2},{2,3},{5,4},{4,5},{7,6},{6,7},{9,8},{8,9},{11,10... | collective-permute-start | bytes 2359304 | tf_op jit(solution)/shard_map/ppermute | solution.py:28
  110.1 24.0 %collective-permute-start.37 = (bf16[2,1024,128]{2,1,0:T(8,128)(2,1)S(1)}, bf16[2,1024,128]{2,1,0:T(8,128)(2,1)S(1)}, u32[]{:S(2)}, u32[]{:S(2)}) collective-permute-start(bf16[2,1024,128]{2,1,0:T(8,128)(2,1)S(1)} %pad_maximum_fusion.6), channel_id=1, source_target_pairs={{24,0},{25,1},{26,2},{27,3},{28,4},{29,5},{30,6},{31,7},{0,8},{1,9... | collective-permute-start | bytes 1572872 | tf_op jit(solution)/shard_map/ppermute | solution.py:28
  134.2 41.7 %collective-permute-start.15 = (s16[272,1024]{1,0:T(8,128)(2,1)S(1)}, s16[272,1024]{1,0:T(8,128)(2,1)S(1)}, u32[]{:S(2)}, u32[]{:S(2)}) collective-permute-start(s16[272,1024]{1,0:T(8,128)(2,1)S(1)} %get-tuple-element.28), channel_id=1, source_target_pairs={{3,0},{2,1},{1,2},{0,3},{7,4},{6,5},{5,6},{4,7},{11,8},{10,9},{9,1... | collective-permute-start | bytes 1671176 | tf_op jit(solution)/shard_map/ppermute | solution.py:28
  136.0 47.7 %collective-permute-start.23 = (s16[272,1024]{1,0:T(8,128)(2,1)S(1)}, s16[272,1024]{1,0:T(8,128)(2,1)S(1)}, u32[]{:S(2)}, u32[]{:S(2)}) collective-permute-start(s16[272,1024]{1,0:T(8,128)(2,1)S(1)} %get-tuple-element.31), channel_id=1, source_target_pairs={{3,0},{2,1},{1,2},{0,3},{7,4},{6,5},{5,6},{4,7},{11,8},{10,9},{9,1... | collective-permute-start | bytes 1671176 | tf_op jit(solution)/shard_map/ppermute | solution.py:28
  140.7 46.0 %collective-permute-start.39 = (s16[272,1024]{1,0:T(8,128)(2,1)S(1)}, s16[272,1024]{1,0:T(8,128)(2,1)S(1)}, u32[]{:S(2)}, u32[]{:S(2)}) collective-permute-start(s16[272,1024]{1,0:T(8,128)(2,1)S(1)} %get-tuple-element.38), channel_id=1, source_target_pairs={{3,0},{2,1},{1,2},{0,3},{7,4},{6,5},{5,6},{4,7},{11,8},{10,9},{9,1... | collective-permute-start | bytes 1671176 | tf_op jit(solution)/shard_map/ppermute | solution.py:28
  145.8 30.0 %collective-permute-start.7 = (s16[272,512]{1,0:T(8,128)(2,1)S(1)}, s16[272,512]{1,0:T(8,128)(2,1)S(1)}, u32[]{:S(2)}, u32[]{:S(2)}) collective-permute-start(s16[272,512]{1,0:T(8,128)(2,1)S(1)} %get-tuple-element.26), channel_id=1, source_target_pairs={{3,0},{2,1},{1,2},{0,3},{7,4},{6,5},{5,6},{4,7},{11,8},{10,9},{9,1... | collective-permute-start | bytes 835592 | tf_op jit(solution)/shard_map/ppermute | solution.py:28
  149.6 34.1 %collective-permute-start.30 = (s16[272,512]{1,0:T(8,128)(2,1)S(1)}, s16[272,512]{1,0:T(8,128)(2,1)S(1)}, u32[]{:S(2)}, u32[]{:S(2)}) collective-permute-start(s16[272,512]{1,0:T(8,128)(2,1)S(1)} %get-tuple-element.33), channel_id=1, source_target_pairs={{3,0},{2,1},{1,2},{0,3},{7,4},{6,5},{5,6},{4,7},{11,8},{10,9},{9,1... | collective-permute-start | bytes 835592 | tf_op jit(solution)/shard_map/ppermute | solution.py:28
  176.2 11.8 %copy-start.2 = (s32[4,64]{1,0:T(4,128)S(1)}, s32[4,64]{1,0:T(4,128)}, u32[]{:S(2)}) copy-start(s32[4,64]{1,0:T(4,128)} %mask_ref.5) | copy-start | bytes 3076
  176.2 10.8 %collective-permute-start.31 = (bf16[128,1536]{1,0:T(8,128)(2,1)S(1)}, bf16[128,1536]{1,0:T(8,128)(2,1)S(1)}, u32[]{:S(2)}, u32[]{:S(2)}) collective-permute-start(bf16[128,1536]{1,0:T(8,128)(2,1)S(1)} %get-tuple-element.35), channel_id=1, source_target_pairs={{4,0},{5,1},{6,2},{7,3},{0,4},{1,5},{2,6},{3,7},{12,8},{13,9},{14,... | collective-permute-start | bytes 1179656 | tf_op jit(solution)/shard_map/ppermute | solution.py:28
  184.1 4.0 %collective-permute-start.32 = (bf16[128,1536]{1,0:T(8,128)(2,1)S(1)}, bf16[128,1536]{1,0:T(8,128)(2,1)S(1)}, u32[]{:S(2)}, u32[]{:S(2)}) collective-permute-start(bf16[128,1536]{1,0:T(8,128)(2,1)S(1)} %get-tuple-element.36), channel_id=1, source_target_pairs={{4,0},{5,1},{6,2},{7,3},{0,4},{1,5},{2,6},{3,7},{12,8},{13,9},{14,... | collective-permute-start | bytes 1179656 | tf_op jit(solution)/shard_map/ppermute | solution.py:28
  186.9 3.6 %collective-permute-start.40 = (bf16[128,1024]{1,0:T(8,128)(2,1)S(1)}, bf16[128,1024]{1,0:T(8,128)(2,1)S(1)}, u32[]{:S(2)}, u32[]{:S(2)}) collective-permute-start(bf16[128,1024]{1,0:T(8,128)(2,1)S(1)} %get-tuple-element.40), channel_id=1, source_target_pairs={{4,0},{5,1},{6,2},{7,3},{0,4},{1,5},{2,6},{3,7},{12,8},{13,9},{14,... | collective-permute-start | bytes 786440 | tf_op jit(solution)/shard_map/ppermute | solution.py:28
